TPU v7x, 256 devices: a whole 4x4x8 slice. The times are simulated.
256 devices in a mesh: gx: 8 (over z), gy: 32 (over x, y, core).
Axes of the slice: x: 4, y: 4, z: 8, core: 2. Of those that a mesh axis runs over, the one named last changes fastest.
Arguments:
- features: bfloat16 [65536, 512], P(('gx', 'gy')), may hold values from -24 to 24
- cotangent: bfloat16 [65536, 512], P(('gx', 'gy')), may hold values from -24 to 24
- self_weight: bfloat16 [3, 512, 512], replicated, may hold values from -0.25 to 0.25
- neigh_weight: bfloat16 [3, 512, 512], replicated, may hold values from -0.25 to 0.25
- block_val: bfloat16 [512, 4, 128, 128], P(('gx', 'gy')), may hold values from -0.25 to 0.25
- block_col: int32 [512, 4], P(('gx', 'gy')), may hold values from 0 to 5
- send_idx: int32 [256, 256, 2], P(('gx', 'gy')), may hold values from 0 to 255
- send_count: int32 [256, 256], P(('gx', 'gy')), may hold values from 0 to 2, as said below
Outputs:
- self_grad: bfloat16 [3, 512, 512], replicated
- neigh_grad: bfloat16 [3, 512, 512], replicated
- input_grad: bfloat16 [65536, 512], P(('gx', 'gy'))
Inputs may be any that keep to these rules, and one draw needn't show every extreme that they name: `send_count`: at most 2 rows from one device to one peer; in every draw some receivers get exactly 2 from every device.
All inputs are finite; a program needn't handle non-finite values.
Results may differ from a plain program's by a relative error of at most 0.02.
Values may be sent and summed in bfloat16 or wider, within the bound.
A program may use at most 128 MiB of HBM per device.

v0:
```python
import math

import jax
import jax.numpy as jnp
from jax import lax
from jax.sharding import PartitionSpec as P


def in_blocks(array, dim, length):
    lengths = array.shape
    tiles = array.reshape(*lengths[:dim], length, lengths[dim] // length, *lengths[dim + 1 :])
    return jnp.moveaxis(tiles, dim, 0)


def in_order(tiles, dim):
    lengths = list(tiles.shape[1:])
    lengths[dim] *= tiles.shape[0]
    return jnp.moveaxis(tiles, 0, dim).reshape(lengths)


def exchange_both(array, axis, axes, splits, concats):
    sizes = [lax.axis_size(a) for a in axes]
    tiles = in_blocks(array, splits[0], sizes[0])
    tiles = jnp.moveaxis(in_blocks(tiles, splits[1] + 1, sizes[1]), 0, 1)
    inside = tiles.shape[2:]
    tiles = tiles.reshape(-1, *inside)
    tiles = lax.all_to_all(tiles, axis, split_axis=0, concat_axis=0, tiled=True)
    tiles = in_order(tiles.reshape(*sizes, *inside), concats[0] + 1)
    return in_order(tiles, concats[1])


def packed_total(arrays, axis):
    vector, at, gathered = (jnp.concatenate([a.reshape(-1) for a in arrays]), 0, [])
    so_far = lax.psum(vector, axis)
    for a in arrays:
        gathered.append(so_far[at : at + a.size].reshape(a.shape))
        at += a.size
    return tuple(gathered)


def gather_sum(extended, values, columns, tile):
    width = extended.shape[1]
    tiled = extended.reshape(-1, tile, width)[columns]
    total = jnp.einsum("rbij,rbjd->rid", values, tiled, preferred_element_type=jnp.float32)
    return total.reshape(-1, width)


def spread_back(upstream, values, columns, ext_tiles, tile):
    width = upstream.shape[1]
    contrib = jnp.einsum(
        "rbij,rid->rbjd",
        values,
        upstream.reshape(-1, tile, width),
        preferred_element_type=jnp.float32,
    )
    onehot = (
        columns.reshape(-1)[None, :] == jnp.arange(ext_tiles, dtype=jnp.int32)[:, None]
    ).astype(jnp.float32)
    total = jnp.einsum(
        "cn,njd->cjd", onehot, contrib.reshape(-1, tile, width), precision=lax.Precision.HIGHEST
    )
    return total.reshape(-1, width)


def per_device(
    features, cotangent, self_weight, neigh_weight, block_val, block_col, send_idx, send_count
):
    outer = lax.axis_size("gx")
    inner = lax.axis_size("gy")
    devices = outer * inner
    node_rows, width = features.shape
    tile = block_val.shape[2]
    layers = self_weight.shape[0]
    slots = send_idx.shape[2]
    halo_rows = devices * slots
    ext_tiles = (node_rows + halo_rows) // tile
    scale = 1.0 / math.sqrt(node_rows * devices)
    row_ids = send_idx.reshape(-1)
    live = (jnp.arange(slots, dtype=jnp.int32)[None, :] < send_count.reshape(-1)[:, None]).reshape(
        -1, 1
    )
    hiddens = [features]
    aggregates = []
    preacts = []
    hidden = features
    for layer_at in range(layers):
        picked = jnp.where(live, jnp.take(hidden, row_ids, axis=0), jnp.zeros((), hidden.dtype))
        picked = picked.reshape(outer, inner, slots, width)
        send_arrived = exchange_both(picked, ("gx", "gy"), ("gx", "gy"), (0, 1), (0, 1))
        extended = jnp.concatenate([hidden, send_arrived.reshape(halo_rows, width)], axis=0)
        aggregate = gather_sum(extended, block_val, block_col, tile).astype(jnp.bfloat16)
        preact = jnp.dot(
            hidden, self_weight[layer_at], preferred_element_type=jnp.float32
        ) + jnp.dot(aggregate, neigh_weight[layer_at], preferred_element_type=jnp.float32)
        aggregates.append(aggregate)
        preacts.append(preact)
        if layer_at < layers - 1:
            hidden = jax.nn.silu(preact).astype(jnp.bfloat16)
            hiddens.append(hidden)
    transposed = (((0,), (0,)), ((), ()))
    against = (((1,), (1,)), ((), ()))
    self_list = [None] * layers
    neigh_list = [None] * layers
    grad = cotangent
    for layer_at in reversed(range(layers)):
        preact = preacts[layer_at]
        sigma = jax.nn.sigmoid(preact)
        delta = (grad.astype(jnp.float32) * sigma * (1.0 + preact * (1.0 - sigma))).astype(
            jnp.bfloat16
        )
        self_term = lax.dot_general(
            hiddens[layer_at], delta, transposed, preferred_element_type=jnp.float32
        )
        neigh_term = lax.dot_general(
            aggregates[layer_at], delta, transposed, preferred_element_type=jnp.float32
        )
        self_sum, neigh_sum = tuple(
            (
                part.astype(jnp.float32)
                for part in packed_total(
                    (self_term.astype(jnp.bfloat16), neigh_term.astype(jnp.bfloat16)), ("gx", "gy")
                )
            )
        )
        self_list[layer_at] = (self_sum * scale).astype(jnp.bfloat16)
        neigh_list[layer_at] = (neigh_sum * scale).astype(jnp.bfloat16)
        own_part = lax.dot_general(
            delta, self_weight[layer_at], against, preferred_element_type=jnp.float32
        )
        upstream = lax.dot_general(
            delta, neigh_weight[layer_at], against, preferred_element_type=jnp.float32
        ).astype(jnp.bfloat16)
        ext_grad = spread_back(upstream, block_val, block_col, ext_tiles, tile)
        outgoing = ext_grad[node_rows:].astype(jnp.bfloat16).reshape(outer, inner, slots, width)
        arrived = exchange_both(outgoing, ("gx", "gy"), ("gx", "gy"), (0, 1), (0, 1))
        masked = jnp.where(
            live, arrived.reshape(halo_rows, width).astype(jnp.float32), jnp.zeros((), jnp.float32)
        )
        returned = jnp.zeros((node_rows, width), jnp.float32).at[row_ids].add(masked)
        grad = (own_part + ext_grad[:node_rows] + returned).astype(jnp.bfloat16)
    self_grad = jnp.stack(self_list)
    neigh_grad = jnp.stack(neigh_list)
    return (self_grad, neigh_grad, grad)


def solution(mesh):
    return jax.shard_map(
        per_device,
        mesh=mesh,
        in_specs=(
            P(("gx", "gy"), None),
            P(("gx", "gy"), None),
            P(),
            P(),
            P(("gx", "gy"), None, None, None),
            P(("gx", "gy"), None),
            P(("gx", "gy"), None, None),
            P(("gx", "gy"), None),
        ),
        out_specs=(P(), P(), P(("gx", "gy"), None)),
        check_vma=False,
    )
```

profile of v0, /device:TPU:1, one launch (start us, length us, event | category | flops | bytes accessed | tf_op | source)
XLA Modules:
  0.0 498.9 jit_solution(5648574006183696624)
XLA Ops:
  12.4 15.6 %all-to-all-start = ((bf16[256,1,1,2,512]{4,3,2,1,0:T(2,128)(2,1)}), bf16[256,1,1,2,512]{4,3,2,1,0:T(2,128)(2,1)S(1)}, u32[]{:S(2)}, u32[]{:S(2)}) async-start(bf16[256,1,1,2,512]{4,3,2,1,0:T(2,128)(2,1)} %bitcast.243), calls=%async_computation | async-start | bytes 1048576 | tf_op jit(solution)/shard_map/all_to_all | solution.py:27
  29.3 18.7 %all-to-all-done = bf16[256,1,1,2,512]{4,3,2,1,0:T(2,128)(2,1)S(1)} async-done(((bf16[256,1,1,2,512]{4,3,2,1,0:T(2,128)(2,1)}), bf16[256,1,1,2,512]{4,3,2,1,0:T(2,128)(2,1)S(1)}, u32[]{:S(2)}, u32[]{:S(2)}) %all-to-all-start) | async-done | bytes 524320 | tf_op jit(solution)/shard_map/all_to_all | solution.py:27
  53.3 2.3 multiply_convert_fusion.10
  58.7 6.1 %all-to-all-start.1 = ((bf16[256,1,1,2,512]{4,3,2,1,0:T(2,128)(2,1)}), bf16[256,1,1,2,512]{4,3,2,1,0:T(2,128)(2,1)S(1)}, u32[]{:S(2)}, u32[]{:S(2)}) async-start(bf16[256,1,1,2,512]{4,3,2,1,0:T(2,128)(2,1)} %bitcast.246), calls=%async_computation.1 | async-start | bytes 1048576 | tf_op jit(solution)/shard_map/all_to_all | solution.py:27
  65.9 18.8 %all-to-all-done.1 = bf16[256,1,1,2,512]{4,3,2,1,0:T(2,128)(2,1)S(1)} async-done(((bf16[256,1,1,2,512]{4,3,2,1,0:T(2,128)(2,1)}), bf16[256,1,1,2,512]{4,3,2,1,0:T(2,128)(2,1)S(1)}, u32[]{:S(2)}, u32[]{:S(2)}) %all-to-all-start.1) | async-done | bytes 524320 | tf_op jit(solution)/shard_map/all_to_all | solution.py:27
  90.1 2.2 multiply_convert_fusion.9
  97.4 6.4 %all-to-all-start.2 = ((bf16[256,1,1,2,512]{4,3,2,1,0:T(2,128)(2,1)}), bf16[256,1,1,2,512]{4,3,2,1,0:T(2,128)(2,1)S(1)}, u32[]{:S(2)}, u32[]{:S(2)}) async-start(bf16[256,1,1,2,512]{4,3,2,1,0:T(2,128)(2,1)} %bitcast.244), calls=%async_computation.2 | async-start | bytes 1048576 | tf_op jit(solution)/shard_map/all_to_all | solution.py:27
  105.1 18.5 %all-to-all-done.2 = bf16[256,1,1,2,512]{4,3,2,1,0:T(2,128)(2,1)S(1)} async-done(((bf16[256,1,1,2,512]{4,3,2,1,0:T(2,128)(2,1)}), bf16[256,1,1,2,512]{4,3,2,1,0:T(2,128)(2,1)S(1)}, u32[]{:S(2)}, u32[]{:S(2)}) %all-to-all-start.2) | async-done | bytes 524320 | tf_op jit(solution)/shard_map/all_to_all | solution.py:27
  132.5 2.7 fusion.55
  138.4 7.4 %all-to-all-start.3 = ((bf16[256,1,1,2,512]{4,3,2,1,0:T(2,128)(2,1)}), bf16[256,1,1,2,512]{4,3,2,1,0:T(2,128)(2,1)}, u32[]{:S(2)}, u32[]{:S(2)}) async-start(bf16[256,1,1,2,512]{4,3,2,1,0:T(2,128)(2,1)} %bitcast.239), calls=%async_computation.3 | async-start | bytes 1048576 | tf_op jit(solution)/shard_map/all_to_all | solution.py:27
  151.1 13.9 %all-to-all-done.3 = bf16[256,1,1,2,512]{4,3,2,1,0:T(2,128)(2,1)} async-done(((bf16[256,1,1,2,512]{4,3,2,1,0:T(2,128)(2,1)}), bf16[256,1,1,2,512]{4,3,2,1,0:T(2,128)(2,1)}, u32[]{:S(2)}, u32[]{:S(2)}) %all-to-all-start.3) | async-done | bytes 524320 | tf_op jit(solution)/shard_map/all_to_all | solution.py:27
  166.2 4.2 scatter_custom_fusion
  174.7 2.1 copy.46
  176.8 2.7 fusion.53
  180.9 6.1 %all-to-all-start.4 = ((bf16[256,1,1,2,512]{4,3,2,1,0:T(2,128)(2,1)}), bf16[256,1,1,2,512]{4,3,2,1,0:T(2,128)(2,1)S(1)}, u32[]{:S(2)}, u32[]{:S(2)}) async-start(bf16[256,1,1,2,512]{4,3,2,1,0:T(2,128)(2,1)} %bitcast.238), calls=%async_computation.4 | async-start | bytes 1048576 | tf_op jit(solution)/shard_map/all_to_all | solution.py:27
  192.3 14.6 %all-to-all-done.4 = bf16[256,1,1,2,512]{4,3,2,1,0:T(2,128)(2,1)S(1)} async-done(((bf16[256,1,1,2,512]{4,3,2,1,0:T(2,128)(2,1)}), bf16[256,1,1,2,512]{4,3,2,1,0:T(2,128)(2,1)S(1)}, u32[]{:S(2)}, u32[]{:S(2)}) %all-to-all-start.4) | async-done | bytes 524320 | tf_op jit(solution)/shard_map/all_to_all | solution.py:27
  207.1 4.2 scatter_custom_fusion.1
  217.8 2.7 fusion.51
  221.9 6.1 %all-to-all-start.5 = ((bf16[256,1,1,2,512]{4,3,2,1,0:T(2,128)(2,1)}), bf16[256,1,1,2,512]{4,3,2,1,0:T(2,128)(2,1)S(1)}, u32[]{:S(2)}, u32[]{:S(2)}) async-start(bf16[256,1,1,2,512]{4,3,2,1,0:T(2,128)(2,1)} %bitcast.242), calls=%async_computation.5 | async-start | bytes 1048576 | tf_op jit(solution)/shard_map/all_to_all | solution.py:27
  229.8 20.0 %all-to-all-done.5 = bf16[256,1,1,2,512]{4,3,2,1,0:T(2,128)(2,1)S(1)} async-done(((bf16[256,1,1,2,512]{4,3,2,1,0:T(2,128)(2,1)}), bf16[256,1,1,2,512]{4,3,2,1,0:T(2,128)(2,1)S(1)}, u32[]{:S(2)}, u32[]{:S(2)}) %all-to-all-start.5) | async-done | bytes 524320 | tf_op jit(solution)/shard_map/all_to_all | solution.py:27
  249.9 3.9 scatter_custom_fusion.2
  254.6 224.4 %all-reduce.3.cloned.1.call-done = (bf16[524288]{0:T(1024)(128)(2,1)}, bf16[524288]{0:T(1024)(128)(2,1)}, bf16[524288]{0:T(1024)(128)(2,1)}) async-done(((bf16[524288]{0:T(1024)(128)(2,1)}, bf16[524288]{0:T(1024)(128)(2,1)}, bf16[524288]{0:T(1024)(128)(2,1)}), (bf16[524288]{0:T(1024)(128)(2,1)}, bf16[524288]{0:T(1024)(128)(2,1)}, bf16[524288]{0:T(1024)(128)(2,1)})) %all-reduce.3.cloned.1.call-update) | async-done | bytes 3145744 | tf_op jit(solution)/shard_map/psum | solution.py:34
  479.0 2.8 multiply_convert_fusion
  485.5 2.2 stack.26
  (130 shorter events, 75.1 us)
Async XLA Ops:
  7.2 44.5 %copy-start = (bf16[2,4,128,128]{3,2,1,0:T(8,128)(2,1)S(1)}, bf16[2,4,128,128]{3,2,1,0:T(8,128)(2,1)}, u32[]{:S(2)}) copy-start(bf16[2,4,128,128]{3,2,1,0:T(8,128)(2,1)} %param.14) | copy-start | bytes 786436
  7.2 2.0 copy-start.1
  11.2 16.9 %copy-start.14 = (s32[2,4]{1,0:T(2,128)S(1)}, s32[2,4]{1,0:T(2,128)}, u32[]{:S(2)}) copy-start(s32[2,4]{1,0:T(2,128)} %param.15) | copy-start | bytes 100
  11.2 17.0 %copy-start.2 = (bf16[3,512,512]{2,1,0:T(8,128)(2,1)S(1)}, bf16[3,512,512]{2,1,0:T(8,128)(2,1)}, u32[]{:S(2)}) copy-start(bf16[3,512,512]{2,1,0:T(8,128)(2,1)} %param.12) | copy-start | bytes 4718596
  12.4 35.6 %all-to-all-start = ((bf16[256,1,1,2,512]{4,3,2,1,0:T(2,128)(2,1)}), bf16[256,1,1,2,512]{4,3,2,1,0:T(2,128)(2,1)S(1)}, u32[]{:S(2)}, u32[]{:S(2)}) async-start(bf16[256,1,1,2,512]{4,3,2,1,0:T(2,128)(2,1)} %bitcast.243), calls=%async_computation | async-start | bytes 1048576 | tf_op jit(solution)/shard_map/all_to_all | solution.py:27
  51.7 1.6 copy-start.11
  53.3 2.3 copy-start.5
  58.7 26.1 %all-to-all-start.1 = ((bf16[256,1,1,2,512]{4,3,2,1,0:T(2,128)(2,1)}), bf16[256,1,1,2,512]{4,3,2,1,0:T(2,128)(2,1)S(1)}, u32[]{:S(2)}, u32[]{:S(2)}) async-start(bf16[256,1,1,2,512]{4,3,2,1,0:T(2,128)(2,1)} %bitcast.246), calls=%async_computation.1 | async-start | bytes 1048576 | tf_op jit(solution)/shard_map/all_to_all | solution.py:27
  88.5 1.6 copy-start.12
  90.1 2.3 copy-start.7
  94.3 9.5 %copy-start.15 = (s32[2,4]{1,0:T(2,128)S(1)}, s32[2,4]{1,0:T(2,128)}, u32[]{:S(2)}) copy-start(s32[2,4]{1,0:T(2,128)} %param.15) | copy-start | bytes 100
  97.4 26.2 %all-to-all-start.2 = ((bf16[256,1,1,2,512]{4,3,2,1,0:T(2,128)(2,1)}), bf16[256,1,1,2,512]{4,3,2,1,0:T(2,128)(2,1)S(1)}, u32[]{:S(2)}, u32[]{:S(2)}) async-start(bf16[256,1,1,2,512]{4,3,2,1,0:T(2,128)(2,1)} %bitcast.244), calls=%async_computation.2 | async-start | bytes 1048576 | tf_op jit(solution)/shard_map/all_to_all | solution.py:27
  123.9 1.0 copy-start.13
  124.5 1.4 copy-start.16
  138.4 26.6 %all-to-all-start.3 = ((bf16[256,1,1,2,512]{4,3,2,1,0:T(2,128)(2,1)}), bf16[256,1,1,2,512]{4,3,2,1,0:T(2,128)(2,1)}, u32[]{:S(2)}, u32[]{:S(2)}) async-start(bf16[256,1,1,2,512]{4,3,2,1,0:T(2,128)(2,1)} %bitcast.239), calls=%async_computation.3 | async-start | bytes 1048576 | tf_op jit(solution)/shard_map/all_to_all | solution.py:27
  165.0 5.4 %copy-start.10 = (f32[256,512]{1,0:T(8,128)S(1)}, f32[256,512]{1,0:T(8,128)}, u32[]{:S(2)}) copy-start(f32[256,512]{1,0:T(8,128)} %get-tuple-element.16) | copy-start | bytes 1572868
  170.4 2.7 copy-start.8
  180.9 26.1 %all-to-all-start.4 = ((bf16[256,1,1,2,512]{4,3,2,1,0:T(2,128)(2,1)}), bf16[256,1,1,2,512]{4,3,2,1,0:T(2,128)(2,1)S(1)}, u32[]{:S(2)}, u32[]{:S(2)}) async-start(bf16[256,1,1,2,512]{4,3,2,1,0:T(2,128)(2,1)} %bitcast.238), calls=%async_computation.4 | async-start | bytes 1048576 | tf_op jit(solution)/shard_map/all_to_all | solution.py:27
  187.0 292.0 %all-reduce.3.cloned.1.call-start = ((), (), s32[]{:S(2)}) async-start(), calls=%async_computation.6 | async-start | bytes 6291456 | tf_op jit(solution)/shard_map/psum | solution.py:34
  207.1 4.2 copy-start.9
  211.3 1.9 copy-start.6
  221.9 27.9 %all-to-all-start.5 = ((bf16[256,1,1,2,512]{4,3,2,1,0:T(2,128)(2,1)}), bf16[256,1,1,2,512]{4,3,2,1,0:T(2,128)(2,1)S(1)}, u32[]{:S(2)}, u32[]{:S(2)}) async-start(bf16[256,1,1,2,512]{4,3,2,1,0:T(2,128)(2,1)} %bitcast.242), calls=%async_computation.5 | async-start | bytes 1048576 | tf_op jit(solution)/shard_map/all_to_all | solution.py:27
  488.8 1.3 copy-start.3
  488.8 1.5 copy-start.4
Sparse Core Ops, SparseCore 0:
  215.4 263.5 all-reduce.2
where the time goes:
time: 508 us; the launch traced here: 499 us
  waiting for transfers between devices  329 us (65%)
  starting transfers between devices  47.9 us (9%)
  local copies, waits for them, and re-layouts  44.6 us (9%)
  matrix products  34.4 us (7%)
  other arithmetic  27.8 us (5%)
  between operations  15.1 us (3%)
    psum x1, waiting for transfers between devices, packed_total(): so_far = lax.psum(vector, axis)  224 us
    all_to_all x6, waiting for transfers between devices, exchange_both(): tiles = lax.all_to_all(tiles, axis, split_axis=0, concat_axis=0, tiled=True)  105 us
    all_to_all x6, starting transfers between devices, exchange_both(): tiles = lax.all_to_all(tiles, axis, split_axis=0, concat_axis=0, tiled=True)  47.9 us
    scatter-add x3, other arithmetic, per_device(): jnp.zeros((node_rows, width), jnp.float32).at[row_ids].add(masked)  12.3 us
  transfers between devices with their start and end apart: 7, of which 7 were waited for; matrix products, arithmetic and copies ran while one was open for 5% of the time, Pallas kernels for 0%

commit v1 on v0

v1 whole, which is shorter than its diff:
```python
import math

import jax
import jax.numpy as jnp
from jax import lax
from jax.experimental import pallas as pl
from jax.experimental.pallas import tpu as pltpu
from jax.sharding import PartitionSpec as P

MESH = pl.DeviceIdType.MESH
LANE = 128


def place():
    z, g = lax.axis_index("gx"), lax.axis_index("gy")
    x, y, c = g // 8, lax.rem(g // 2, 4), lax.rem(g, 2)
    return z, x, y, c


def flip(p, kind):
    return p + 1 - 2 * lax.rem(p, 2) if kind == 0 else 3 - p


def kept(p, kind):
    return lax.rem((p + 1) // 2, 2) if kind == 0 else p // 2


def rows(start, size):
    return pl.ds(pl.multiple_of(start, 16), size)


STEPS = (
    (("x", 0), ("x", 1), ("y", 0), ("y", 1)),
    (("x", 1), ("x", 0), ("y", 1), ("y", 0)),
    (("y", 0), ("y", 1), ("x", 0), ("x", 1)),
    (("y", 1), ("y", 0), ("x", 1), ("x", 0)),
)


def sum_kernel(
    scale, g_ref, out_ref, full, part, other, got, back, zin, zout, zgot, zall, ssem, rsem, zs, zr
):
    z, x, y, c = place()
    zn = 8
    n_mat, width = g_ref.shape[0], g_ref.shape[1]
    total = full.shape[0]
    half = total // 2
    colour = half // 4

    def at(x_, y_, c_):
        return (z, x_ * 8 + y_ * 2 + c_)

    def partner(axis, kind):
        return at(flip(x, kind), y, c) if axis == "x" else at(x, flip(y, kind), c)

    def keep(axis, kind):
        return kept(x if axis == "x" else y, kind)

    twin = at(x, y, 1 - c)
    bar = pltpu.get_barrier_semaphore()
    peers = [twin] + [partner(a, k) for a in "xy" for k in (0, 1)]
    peers += [(lax.rem(z + d, zn), x * 8 + y * 2 + c) for d in range(1, zn)]
    for peer in peers:
        pl.semaphore_signal(bar, inc=1, device_id=peer, device_id_type=MESH)

    blocks = width // LANE

    def load(i, carry):
        for k in range(blocks):
            full[rows((i * blocks + k) * width, width), :] = g_ref[
                i, :, k * LANE : (k + 1) * LANE
            ]
        return carry

    lax.fori_loop(0, n_mat, load, 0)
    pl.semaphore_wait(bar, len(peers))

    def copy(src, dst, s, r, peer):
        return pltpu.make_async_remote_copy(
            src_ref=src, dst_ref=dst, send_sem=s, recv_sem=r, device_id=peer, device_id_type=MESH
        )

    sends = []

    def go(*args):
        move = copy(*args)
        move.start()
        sends.append(move)

    for q in range(4):
        src = full.at[rows((1 - c) * half + q * colour, colour)]
        go(src, other.at[pl.ds(q * colour, colour)], ssem.at[q], rsem.at[q], twin)

    def add(dst, base, a, a_base, b, b_base, size):
        step = 96

        def body(i, carry):
            at_a = rows(a_base + i * step, step)
            at_b = rows(b_base + i * step, step)
            s = a[at_a, :].astype(jnp.float32) + b[at_b, :].astype(jnp.float32)
            dst[rows(base + i * step, step), :] = s.astype(jnp.bfloat16)
            return carry

        lax.fori_loop(0, size // step, body, 0)

    offset = [None] * 4
    got_at = [0, 4 * 768, 4 * 768 + 4 * 384, 4 * 768 + 4 * 384 + 4 * 192]

    for q in range(4):
        here = other.at[pl.ds(q * colour, colour)]
        copy(here, here, ssem.at[q], rsem.at[q], twin).wait_recv()
        add(part, q * colour, full, c * half + q * colour, other, q * colour, colour)
        offset[q] = q * colour
        axis, kind = STEPS[q][0]
        size = colour // 2
        k = keep(axis, kind)
        go(
            part.at[rows(offset[q] + (1 - k) * size, size)],
            got.at[pl.ds(got_at[0] + q * size, size)],
            ssem.at[4 + q],
            rsem.at[4 + q],
            partner(axis, kind),
        )
        offset[q] = offset[q] + k * size

    for step in range(4):
        size = colour >> (step + 1)
        for q in range(4):
            axis, kind = STEPS[q][step]
            here = got.at[pl.ds(got_at[step] + q * size, size)]
            sem = 4 + 4 * step + q
            copy(here, here, ssem.at[sem], rsem.at[sem], partner(axis, kind)).wait_recv()
            add(part, offset[q], part, offset[q], got, got_at[step] + q * size, size)
            if step < 3:
                axis, kind = STEPS[q][step + 1]
                nxt = size // 2
                k = keep(axis, kind)
                go(
                    part.at[rows(offset[q] + (1 - k) * nxt, nxt)],
                    got.at[pl.ds(got_at[step + 1] + q * nxt, nxt)],
                    ssem.at[sem + 4],
                    rsem.at[sem + 4],
                    partner(axis, kind),
                )
                offset[q] = offset[q] + k * nxt

    last = colour >> 4
    for q in range(4):
        zin[q * last : (q + 1) * last, :] = part[rows(offset[q], last), :]
    piece = 4 * last // zn
    for d in range(1, zn):
        to = lax.rem(z + d, zn)
        go(
            zin.at[rows(to * piece, piece)],
            zgot.at[pl.ds((d - 1) * piece, piece)],
            zs.at[d - 1],
            zr.at[d - 1],
            (to, x * 8 + y * 2 + c),
        )
    run = zin[rows(z * piece, piece), :].astype(jnp.float32)
    for d in range(1, zn):
        here = zgot.at[pl.ds((d - 1) * piece, piece)]
        copy(here, here, zs.at[d - 1], zr.at[d - 1], twin).wait_recv()
        run = run + zgot[(d - 1) * piece : d * piece, :].astype(jnp.float32)
    zout[...] = run.astype(jnp.bfloat16)
    for d in range(1, zn):
        to = lax.rem(z + d, zn)
        go(
            zout,
            zall.at[rows(z * piece, piece)],
            zs.at[zn - 1 + d - 1],
            zr.at[zn - 1 + d - 1],
            (to, x * 8 + y * 2 + c),
        )
    zall[rows(z * piece, piece), :] = zout[...]
    for d in range(1, zn):
        here = zall.at[pl.ds(0, piece)]
        copy(here, here, zs.at[0], zr.at[zn - 1 + d - 1], twin).wait_recv()
    for step in range(3, -2, -1):
        for q in range(4):
            if step == 3:
                got[rows(got_at[3] + 4 * last + offset[q], last), :] = zall[
                    q * last : (q + 1) * last, :
                ]
            if step >= 0:
                size = colour >> (step + 1)
                if step < 3:
                    axis, kind = STEPS[q][step + 1]
                    sem = 20 + 4 * (step + 1) + q
                    prev = size // 2
                    here = got.at[pl.ds(0, prev)]
                    copy(here, here, ssem.at[sem], rsem.at[sem], twin).wait_recv()
                    offset[q] = offset[q] - keep(axis, kind) * prev
                axis, kind = STEPS[q][step]
                sem = 20 + 4 * step + q
                here = got.at[rows(got_at[3] + 4 * last + offset[q], size)]
                go(here, here, ssem.at[sem], rsem.at[sem], partner(axis, kind))
            else:
                sem = 20 + q
                size = colour // 2
                here = got.at[pl.ds(0, size)]
                copy(here, here, ssem.at[sem], rsem.at[sem], twin).wait_recv()
                base = got_at[3] + 4 * last + q * colour
                here = got.at[pl.ds(base, colour)]
                there = back.at[pl.ds(q * colour, colour)]
                go(here, there, ssem.at[36 + q], rsem.at[36 + q], twin)

    def result(value):
        return (value.astype(jnp.float32) * scale).astype(out_ref.dtype)

    per = n_mat // 2
    base = got_at[3] + 4 * last

    def mine(i, carry):
        for k in range(blocks):
            src = got[rows(base + (i * blocks + k) * width, width), :]
            out_ref[c * per + i, :, k * LANE : (k + 1) * LANE] = result(src)
        return carry

    lax.fori_loop(0, per, mine, 0)
    for q in range(4):
        here = back.at[pl.ds(q * colour, colour)]
        copy(here, here, ssem.at[36 + q], rsem.at[36 + q], twin).wait_recv()

    def theirs(i, carry):
        for k in range(blocks):
            src = back[rows((i * blocks + k) * width, width), :]
            out_ref[(1 - c) * per + i, :, k * LANE : (k + 1) * LANE] = result(src)
        return carry

    lax.fori_loop(0, per, theirs, 0)
    for move in sends:
        move.wait_send()


def total_over_all(grads, scale):
    n_mat, width, _ = grads.shape
    total = n_mat * width * width // LANE
    half = total // 2
    dma = pltpu.SemaphoreType.DMA
    bf = jnp.bfloat16

    def kernel(*refs):
        sum_kernel(scale, *refs)

    return pl.pallas_call(
        kernel,
        out_shape=jax.ShapeDtypeStruct(grads.shape, bf),
        in_specs=[pl.BlockSpec(memory_space=pltpu.VMEM)],
        out_specs=pl.BlockSpec(memory_space=pltpu.VMEM),
        scratch_shapes=[
            pltpu.VMEM((total, LANE), bf),
            pltpu.VMEM((half, LANE), bf),
            pltpu.VMEM((half, LANE), bf),
            pltpu.VMEM((half * 15 // 16 + half, LANE), bf),
            pltpu.VMEM((half, LANE), bf),
            pltpu.VMEM((half // 16, LANE), bf),
            pltpu.VMEM((half // 128, LANE), bf),
            pltpu.VMEM((half // 128 * 7, LANE), bf),
            pltpu.VMEM((half // 16, LANE), bf),
            dma((40,)),
            dma((40,)),
            dma((14,)),
            dma((14,)),
        ],
        compiler_params=pltpu.CompilerParams(
            collective_id=0, has_side_effects=True, vmem_limit_bytes=60 * 1024 * 1024
        ),
        name="sum_over_all",
    )(grads)


def per_device(
    features, cotangent, self_weight, neigh_weight, block_val, block_col, send_idx, send_count
):
    outer = lax.axis_size("gx")
    inner = lax.axis_size("gy")
    devices = outer * inner
    node_rows, width = features.shape
    tile = block_val.shape[2]
    layers = self_weight.shape[0]
    slots = send_idx.shape[2]
    halo_rows = devices * slots
    ext_tiles = (node_rows + halo_rows) // tile
    scale = 1.0 / math.sqrt(node_rows * devices)
    bf, f32 = jnp.bfloat16, jnp.float32
    row_ids = send_idx.reshape(-1)
    live = (jnp.arange(slots, dtype=jnp.int32)[None, :] < send_count.reshape(-1)[:, None]).reshape(
        -1, 1
    )
    pick = ((row_ids[:, None] == jnp.arange(node_rows, dtype=jnp.int32)[None, :]) & live).astype(bf)
    where = (block_col[:, :, None] == jnp.arange(ext_tiles, dtype=jnp.int32)).astype(f32)
    dense = jnp.sum(
        where[:, :, None, :, None] * block_val.astype(f32)[:, :, :, None, :], axis=1
    ).reshape(node_rows, ext_tiles * tile).astype(bf)
    near, far = dense[:, :node_rows], dense[:, node_rows:]
    transposed = (((0,), (0,)), ((), ()))
    against = (((1,), (1,)), ((), ()))

    def dot(a, b, dims=(((1,), (0,)), ((), ()))):
        return lax.dot_general(a, b, dims, preferred_element_type=f32)

    def exchange(array):
        tiles = array.reshape(devices, slots, width)
        tiles = lax.all_to_all(tiles, ("gx", "gy"), split_axis=0, concat_axis=0, tiled=True)
        return tiles.reshape(halo_rows, width)

    hiddens, aggregates, preacts = [features], [], []
    hidden = features
    for layer_at in range(layers):
        arrived = exchange(dot(pick, hidden).astype(bf))
        aggregate = (dot(near, hidden) + dot(far, arrived)).astype(bf)
        preact = dot(hidden, self_weight[layer_at]) + dot(aggregate, neigh_weight[layer_at])
        aggregates.append(aggregate)
        preacts.append(preact)
        if layer_at < layers - 1:
            hidden = jax.nn.silu(preact).astype(bf)
            hiddens.append(hidden)
    terms = [None] * (2 * layers)
    grad = cotangent
    for layer_at in reversed(range(layers)):
        preact = preacts[layer_at]
        sigma = jax.nn.sigmoid(preact)
        delta = (grad.astype(f32) * sigma * (1.0 + preact * (1.0 - sigma))).astype(bf)
        terms[layer_at] = dot(hiddens[layer_at], delta, transposed).astype(bf)
        terms[layers + layer_at] = dot(aggregates[layer_at], delta, transposed).astype(bf)
        upstream = dot(delta, neigh_weight[layer_at], against).astype(bf)
        arrived = exchange(dot(far, upstream, transposed).astype(bf))
        own = dot(delta, self_weight[layer_at], against) + dot(near, upstream, transposed)
        grad = (own + dot(pick, arrived, transposed)).astype(bf)
    sums = total_over_all(jnp.stack(terms), scale)
    return (sums[:layers], sums[layers:], grad)


def solution(mesh):
    return jax.shard_map(
        per_device,
        mesh=mesh,
        in_specs=(
            P(("gx", "gy"), None),
            P(("gx", "gy"), None),
            P(),
            P(),
            P(("gx", "gy"), None, None, None),
            P(("gx", "gy"), None),
            P(("gx", "gy"), None, None),
            P(("gx", "gy"), None),
        ),
        out_specs=(P(), P(), P(("gx", "gy"), None)),
        check_vma=False,
    )
```

time: 508 us -> 263 us (0.52); the launches traced: 499 us -> 262 us
  waiting for transfers between devices: 329 us -> 91.5 us
  Pallas kernels: 0 us -> 64.8 us
  other arithmetic: 27.8 us -> 1.26 us
  local copies, waits for them, and re-layouts: 44.6 us -> 19.5 us
  between operations: 15.1 us -> 1.12 us
    psum x1 -> x0, waiting for transfers between devices: 224 us -> none  [packed_total(): so_far = lax.psum(vector, axis)]
    pallas_call x0 -> x1, Pallas kernels: none -> 64.8 us  [total_over_all(): pl.pallas_call(kernel, out_shape=jax.ShapeDtypeStruct(grads.shape, bf), i...]
    all_to_all x6, waiting for transfers between devices: 105 us -> 91.5 us  [exchange(): lax.all_to_all(tiles, ('gx', 'gy'), split_axis=0, concat_axis=0, tiled=True)]
    scatter-add x3 -> x0, other arithmetic: 12.3 us -> none  [per_device(): jnp.zeros((node_rows, width), jnp.float32).at[row_ids].add(masked)]
    another operation x12 -> x0, local copies, waits for them, and re-layouts: 11.8 us -> none  [the longest x3 4.62 us: per_device(): self_grad = jnp.stack(self_list)]
    gather x6 -> x0, local copies, waits for them, and re-layouts: 9.68 us -> none  [the longest x3 5.9 us: per_device(): jnp.take(hidden, row_ids, axis=0)]
    concatenate x6 -> x0, other arithmetic: 5.37 us -> none  [the longest x3 3.13 us: packed_total(): jnp.concatenate([a.reshape(-1) for a in arrays])]
    convert_element_type x5 -> x2, other arithmetic: 5.34 us -> 0.11 us  [the longest x1 0.07 us: per_device(): (block_col[:, :, None] == jnp.arange(ext_tiles, dtype=jnp.int32)).astype(...]
  transfers between devices with their start and end apart: 7 -> 6, of which waited for: 7 -> 5; matrix products, arithmetic and copies ran while one was open for 5% -> 8% of each run, Pallas kernels for 0% -> 25%
where the time goes in v1:
time: 263 us; the launch traced here: 262 us
  waiting for transfers between devices  91.5 us (35%)
  Pallas kernels  64.8 us (25%)
  starting transfers between devices  46.3 us (18%)
  matrix products  37.2 us (14%)
  local copies, waits for them, and re-layouts  19.5 us (7%)
    all_to_all x6, waiting for transfers between devices, exchange(): lax.all_to_all(tiles, ('gx', 'gy'), split_axis=0, concat_axis=0, tiled=True)  91.5 us
    pallas_call x1, Pallas kernels, total_over_all(): pl.pallas_call(kernel, out_shape=jax.ShapeDtypeStruct(grads.shape, bf), i...  64.8 us
    all_to_all x6, starting transfers between devices, exchange(): lax.all_to_all(tiles, ('gx', 'gy'), split_axis=0, concat_axis=0, tiled=True)  46.3 us
    dot_general x36, matrix products, dot(): return lax.dot_general(a, b, dims, preferred_element_type=f32)  37.2 us
    reshape x6, local copies, waits for them, and re-layouts, exchange(): tiles = array.reshape(devices, slots, width)  6.01 us
  transfers between devices with their start and end apart: 6, of which 5 were waited for; matrix products, arithmetic and copies ran while one was open for 8% of the time, Pallas kernels for 25%

profile of v1, /device:TPU:1, one launch (start us, length us, event | category | flops | bytes accessed | tf_op | source)
XLA Modules:
  0.0 261.7 jit_solution(15618498369569570156)
XLA Ops:
  4.0 15.6 %all-to-all-start = ((bf16[256,2,512]{2,1,0:T(2,128)(2,1)}), bf16[256,2,512]{2,1,0:T(2,128)(2,1)S(1)}, u32[]{:S(2)}, u32[]{:S(2)}) async-start(bf16[256,2,512]{2,1,0:T(2,128)(2,1)} %reshape.67), calls=%async_computation | async-start | bytes 1048576 | tf_op jit(solution)/shard_map/all_to_all | solution.py:305
  23.4 16.2 %all-to-all-done = bf16[256,2,512]{2,1,0:T(2,128)(2,1)S(1)} async-done(((bf16[256,2,512]{2,1,0:T(2,128)(2,1)}), bf16[256,2,512]{2,1,0:T(2,128)(2,1)S(1)}, u32[]{:S(2)}, u32[]{:S(2)}) %all-to-all-start) | async-done | bytes 524320 | tf_op jit(solution)/shard_map/all_to_all | solution.py:305
  40.9 2.2 multiply_convert_fusion.2
  44.5 6.1 %all-to-all-start.1 = ((bf16[256,2,512]{2,1,0:T(2,128)(2,1)}), bf16[256,2,512]{2,1,0:T(2,128)(2,1)S(1)}, u32[]{:S(2)}, u32[]{:S(2)}) async-start(bf16[256,2,512]{2,1,0:T(2,128)(2,1)} %reshape.69), calls=%async_computation.1 | async-start | bytes 1048576 | tf_op jit(solution)/shard_map/all_to_all | solution.py:305
  51.7 18.8 %all-to-all-done.1 = bf16[256,2,512]{2,1,0:T(2,128)(2,1)S(1)} async-done(((bf16[256,2,512]{2,1,0:T(2,128)(2,1)}), bf16[256,2,512]{2,1,0:T(2,128)(2,1)S(1)}, u32[]{:S(2)}, u32[]{:S(2)}) %all-to-all-start.1) | async-done | bytes 524320 | tf_op jit(solution)/shard_map/all_to_all | solution.py:305
  71.8 2.2 multiply_convert_fusion.1
  75.4 6.1 %all-to-all-start.2 = ((bf16[256,2,512]{2,1,0:T(2,128)(2,1)}), bf16[256,2,512]{2,1,0:T(2,128)(2,1)S(1)}, u32[]{:S(2)}, u32[]{:S(2)}) async-start(bf16[256,2,512]{2,1,0:T(2,128)(2,1)} %reshape.71), calls=%async_computation.2 | async-start | bytes 1048576 | tf_op jit(solution)/shard_map/all_to_all | solution.py:305
  82.6 18.8 %all-to-all-done.2 = bf16[256,2,512]{2,1,0:T(2,128)(2,1)S(1)} async-done(((bf16[256,2,512]{2,1,0:T(2,128)(2,1)}), bf16[256,2,512]{2,1,0:T(2,128)(2,1)S(1)}, u32[]{:S(2)}, u32[]{:S(2)}) %all-to-all-start.2) | async-done | bytes 524320 | tf_op jit(solution)/shard_map/all_to_all | solution.py:305
  102.5 1.5 fusion.86
  104.3 1.5 multiply_convert_fusion
  108.2 6.1 %all-to-all-start.3 = ((bf16[256,2,512]{2,1,0:T(2,128)(2,1)}), bf16[256,2,512]{2,1,0:T(2,128)(2,1)S(1)}, u32[]{:S(2)}, u32[]{:S(2)}) async-start(bf16[256,2,512]{2,1,0:T(2,128)(2,1)} %reshape.73), calls=%async_computation.3 | async-start | bytes 1048576 | tf_op jit(solution)/shard_map/all_to_all | solution.py:305
  115.5 18.8 %all-to-all-done.3 = bf16[256,2,512]{2,1,0:T(2,128)(2,1)S(1)} async-done(((bf16[256,2,512]{2,1,0:T(2,128)(2,1)}), bf16[256,2,512]{2,1,0:T(2,128)(2,1)S(1)}, u32[]{:S(2)}, u32[]{:S(2)}) %all-to-all-start.3) | async-done | bytes 524320 | tf_op jit(solution)/shard_map/all_to_all | solution.py:305
  135.3 1.5 fusion.54
  136.8 1.6 fusion.19
  138.4 1.5 convolution_convert_fusion.13
  141.9 6.1 %all-to-all-start.4 = ((bf16[256,2,512]{2,1,0:T(2,128)(2,1)}), bf16[256,2,512]{2,1,0:T(2,128)(2,1)S(1)}, u32[]{:S(2)}, u32[]{:S(2)}) async-start(bf16[256,2,512]{2,1,0:T(2,128)(2,1)} %reshape.75), calls=%async_computation.4 | async-start | bytes 1048576 | tf_op jit(solution)/shard_map/all_to_all | solution.py:305
  149.2 18.8 %all-to-all-done.4 = bf16[256,2,512]{2,1,0:T(2,128)(2,1)S(1)} async-done(((bf16[256,2,512]{2,1,0:T(2,128)(2,1)}), bf16[256,2,512]{2,1,0:T(2,128)(2,1)S(1)}, u32[]{:S(2)}, u32[]{:S(2)}) %all-to-all-start.4) | async-done | bytes 524320 | tf_op jit(solution)/shard_map/all_to_all | solution.py:305
  169.0 1.5 fusion.52
  170.5 1.5 fusion.24
  176.0 6.1 %all-to-all-start.5 = ((bf16[256,2,512]{2,1,0:T(2,128)(2,1)}), bf16[256,2,512]{2,1,0:T(2,128)(2,1)S(1)}, u32[]{:S(2)}, u32[]{:S(2)}) async-start(bf16[256,2,512]{2,1,0:T(2,128)(2,1)} %reshape.77), calls=%async_computation.5 | async-start | bytes 1048576 | tf_op jit(solution)/shard_map/all_to_all | solution.py:305
  182.2 2.2 fusion.3
  184.4 2.1 fusion.5
  189.9 64.8 %sum_over_all.1 = bf16[6,512,512]{2,1,0:T(8,128)(2,1)} custom-call(bf16[6,512,512]{2,1,0:T(8,128)(2,1)} %fusion.11.refs_0_), custom_call_target="tpu_custom_call" | custom-call | tf_op jit(solution)/shard_map/sum_over_all/pallas_call | solution.py:246
  255.8 3.9 %fusion.99 = (bf16[3,512,512]{2,1,0:T(8,128)(2,1)}, bf16[3,512,512]{2,1,0:T(8,128)(2,1)}) fusion(bf16[6,512,512]{2,1,0:T(8,128)(2,1)} %sum_over_all.1), kind=kLoop, calls=%fused_computation.125 | loop fusion | bytes 6291456 | tf_op jit(solution)/shard_map/slice | solution.py:332
  (95 shorter events, 34.6 us)
Async XLA Ops:
  0.6 2.0 copy-start
  1.6 18.0 %copy-start.6 = (bf16[2,4,128,128]{3,2,1,0:T(8,128)(2,1)S(1)}, bf16[2,4,128,128]{3,2,1,0:T(8,128)(2,1)}, u32[]{:S(2)}) copy-start(bf16[2,4,128,128]{3,2,1,0:T(8,128)(2,1)} %param.12) | copy-start | bytes 786436
  3.0 16.7 %copy-start.22 = (s32[2,4]{1,0:T(2,128)S(1)}, s32[2,4]{1,0:T(2,128)}, u32[]{:S(2)}) copy-start(s32[2,4]{1,0:T(2,128)} %param.13) | copy-start | bytes 100
  4.0 35.6 %all-to-all-start = ((bf16[256,2,512]{2,1,0:T(2,128)(2,1)}), bf16[256,2,512]{2,1,0:T(2,128)(2,1)S(1)}, u32[]{:S(2)}, u32[]{:S(2)}) async-start(bf16[256,2,512]{2,1,0:T(2,128)(2,1)} %reshape.67), calls=%async_computation | async-start | bytes 1048576 | tf_op jit(solution)/shard_map/all_to_all | solution.py:305
  19.7 2.6 %copy-start.1 = (bf16[3,512,512]{2,1,0:T(8,128)(2,1)S(1)}, bf16[3,512,512]{2,1,0:T(8,128)(2,1)}, u32[]{:S(2)}) copy-start(bf16[3,512,512]{2,1,0:T(8,128)(2,1)} %param.10) | copy-start | bytes 4718596
  40.9 2.2 copy-start.13
  44.5 26.1 %all-to-all-start.1 = ((bf16[256,2,512]{2,1,0:T(2,128)(2,1)}), bf16[256,2,512]{2,1,0:T(2,128)(2,1)S(1)}, u32[]{:S(2)}, u32[]{:S(2)}) async-start(bf16[256,2,512]{2,1,0:T(2,128)(2,1)} %reshape.69), calls=%async_computation.1 | async-start | bytes 1048576 | tf_op jit(solution)/shard_map/all_to_all | solution.py:305
  71.8 2.2 copy-start.15
  75.4 26.1 %all-to-all-start.2 = ((bf16[256,2,512]{2,1,0:T(2,128)(2,1)}), bf16[256,2,512]{2,1,0:T(2,128)(2,1)S(1)}, u32[]{:S(2)}, u32[]{:S(2)}) async-start(bf16[256,2,512]{2,1,0:T(2,128)(2,1)} %reshape.71), calls=%async_computation.2 | async-start | bytes 1048576 | tf_op jit(solution)/shard_map/all_to_all | solution.py:305
  102.5 1.8 copy-start.5
  102.5 1.8 copy-start.23
  104.3 1.5 copy-start.17
  105.8 8.5 %copy-start.7 = (bf16[256,512]{1,0:T(8,128)(2,1)}, bf16[256,512]{1,0:T(8,128)(2,1)S(1)}, u32[]{:S(2)}) copy-start(bf16[256,512]{1,0:T(8,128)(2,1)S(1)} %multiply_convert_fusion) | copy-start | bytes 786436
  108.2 26.1 %all-to-all-start.3 = ((bf16[256,2,512]{2,1,0:T(2,128)(2,1)}), bf16[256,2,512]{2,1,0:T(2,128)(2,1)S(1)}, u32[]{:S(2)}, u32[]{:S(2)}) async-start(bf16[256,2,512]{2,1,0:T(2,128)(2,1)} %reshape.73), calls=%async_computation.3 | async-start | bytes 1048576 | tf_op jit(solution)/shard_map/all_to_all | solution.py:305
  138.4 9.6 %copy-start.9 = (bf16[256,512]{1,0:T(8,128)(2,1)}, bf16[256,512]{1,0:T(8,128)(2,1)S(1)}, u32[]{:S(2)}) copy-start(bf16[256,512]{1,0:T(8,128)(2,1)S(1)} %fusion.19) | copy-start | bytes 786436
  141.9 26.1 %all-to-all-start.4 = ((bf16[256,2,512]{2,1,0:T(2,128)(2,1)}), bf16[256,2,512]{2,1,0:T(2,128)(2,1)S(1)}, u32[]{:S(2)}, u32[]{:S(2)}) async-start(bf16[256,2,512]{2,1,0:T(2,128)(2,1)} %reshape.75), calls=%async_computation.4 | async-start | bytes 1048576 | tf_op jit(solution)/shard_map/all_to_all | solution.py:305
  149.2 21.3 %copy-start.21 = (bf16[256,512]{1,0:T(8,128)(2,1)S(1)}, bf16[256,512]{1,0:T(8,128)(2,1)}, u32[]{:S(2)}) copy-start(bf16[256,512]{1,0:T(8,128)(2,1)} %copy-done.20) | copy-start | bytes 786436
  176.0 83.7 %all-to-all-start.5 = ((bf16[256,2,512]{2,1,0:T(2,128)(2,1)}), bf16[256,2,512]{2,1,0:T(2,128)(2,1)S(1)}, u32[]{:S(2)}, u32[]{:S(2)}) async-start(bf16[256,2,512]{2,1,0:T(2,128)(2,1)} %reshape.77), calls=%async_computation.5 | async-start | bytes 1048576 | tf_op jit(solution)/shard_map/all_to_all | solution.py:305
  182.2 4.3 %copy-start.12 = (bf16[256,512]{1,0:T(8,128)(2,1)S(1)}, bf16[256,512]{1,0:T(8,128)(2,1)}, u32[]{:S(2)}) copy-start(bf16[256,512]{1,0:T(8,128)(2,1)} %copy-done.11) | copy-start | bytes 786436
  182.2 4.3 %copy-start.14 = (bf16[256,512]{1,0:T(8,128)(2,1)S(1)}, bf16[256,512]{1,0:T(8,128)(2,1)}, u32[]{:S(2)}) copy-start(bf16[256,512]{1,0:T(8,128)(2,1)} %copy-done.13) | copy-start | bytes 786436
  182.2 5.4 %copy-start.10 = (bf16[256,512]{1,0:T(8,128)(2,1)S(1)}, bf16[256,512]{1,0:T(8,128)(2,1)}, u32[]{:S(2)}) copy-start(bf16[256,512]{1,0:T(8,128)(2,1)} %copy-done.9) | copy-start | bytes 786436
  182.2 5.4 %copy-start.16 = (bf16[256,512]{1,0:T(8,128)(2,1)S(1)}, bf16[256,512]{1,0:T(8,128)(2,1)}, u32[]{:S(2)}) copy-start(bf16[256,512]{1,0:T(8,128)(2,1)} %copy-done.15) | copy-start | bytes 786436
  184.4 4.4 %copy-start.8 = (bf16[256,512]{1,0:T(8,128)(2,1)S(1)}, bf16[256,512]{1,0:T(8,128)(2,1)}, u32[]{:S(2)}) copy-start(bf16[256,512]{1,0:T(8,128)(2,1)} %copy-done.7) | copy-start | bytes 786436
  184.4 4.4 %copy-start.18 = (bf16[256,512]{1,0:T(8,128)(2,1)S(1)}, bf16[256,512]{1,0:T(8,128)(2,1)}, u32[]{:S(2)}) copy-start(bf16[256,512]{1,0:T(8,128)(2,1)} %copy-done.17) | copy-start | bytes 786436
  (6 other events, 6.0 us)

commit v2 on v0

v2 whole, which is shorter than its diff:
```python
import math

import jax
import jax.numpy as jnp
from jax import lax
from jax.experimental import pallas as pl
from jax.experimental.pallas import tpu as pltpu
from jax.sharding import PartitionSpec as P

MESH = pl.DeviceIdType.MESH
LANE = 128
BF, F32 = jnp.bfloat16, jnp.float32
ROWS = (((1,), (0,)), ((), ()))
TRANSPOSED = (((0,), (0,)), ((), ()))
AGAINST = (((1,), (1,)), ((), ()))


def dot(a, b, dims=ROWS):
    return lax.dot_general(a, b, dims, preferred_element_type=F32)


def place():
    z, g = lax.axis_index("gx"), lax.axis_index("gy")
    x, y, c = g // 8, lax.rem(g // 2, 4), lax.rem(g, 2)
    return z, g, x, y, c


def flip(p, kind):
    return p + 1 - 2 * lax.rem(p, 2) if kind == 0 else 3 - p


def kept(p, kind):
    return lax.rem((p + 1) // 2, 2) if kind == 0 else p // 2


def rows(start, size):
    return pl.ds(pl.multiple_of(start, 16), size)


def copy(src, dst, s, r, peer):
    return pltpu.make_async_remote_copy(
        src_ref=src, dst_ref=dst, send_sem=s, recv_sem=r, device_id=peer, device_id_type=MESH
    )


STEPS = (
    (("x", 0), ("x", 1), ("y", 0), ("y", 1)),
    (("x", 1), ("x", 0), ("y", 1), ("y", 0)),
    (("y", 0), ("y", 1), ("x", 0), ("x", 1)),
    (("y", 1), ("y", 0), ("x", 1), ("x", 0)),
)
ZN, GN = 8, 32


def sum_stages(layer, scale, outs, bufs, sems, sends):
    z, g, x, y, c = place()
    full, part, other, got, gath, back, zin, zout, zgot, zall = (b.at[layer] for b in bufs)
    ssem, rsem, zs, zr = (s.at[layer] for s in sems)
    half = part.shape[0]
    colour = half // 4

    def at(x_, y_, c_):
        return (z, x_ * 8 + y_ * 2 + c_)

    def partner(axis, kind):
        return at(flip(x, kind), y, c) if axis == "x" else at(x, flip(y, kind), c)

    def keep(axis, kind):
        return kept(x if axis == "x" else y, kind)

    twin = at(x, y, 1 - c)

    def go(*args):
        move = copy(*args)
        move.start()
        sends.append(move)

    def arrive(ref, start, size, sem):
        here = ref.at[pl.ds(start, size)]
        copy(here, here, zs.at[0], sem, twin).wait_recv()

    def add(dst, base, a, a_base, b, b_base, size):
        s = a[rows(a_base, size), :].astype(F32) + b[pl.ds(b_base, size), :].astype(F32)
        dst[rows(base, size), :] = s.astype(BF)

    offset = [q * colour for q in range(4)]
    got_at = [0, 2 * colour, 3 * colour, 3 * colour + colour // 2]

    def halve(q, step):
        axis, kind = STEPS[q][step]
        size = colour >> (step + 1)
        k = keep(axis, kind)
        go(
            part.at[rows(offset[q] + (1 - k) * size, size)],
            got.at[pl.ds(got_at[step] + q * size, size)],
            ssem.at[4 + 4 * step + q],
            rsem.at[4 + 4 * step + q],
            partner(axis, kind),
        )
        offset[q] = offset[q] + k * size

    for q in range(4):
        src = full.at[rows((1 - c) * half + q * colour, colour)]
        go(src, other.at[pl.ds(q * colour, colour)], ssem.at[q], rsem.at[q], twin)
    yield
    for q in range(4):
        arrive(other, q * colour, colour, rsem.at[q])
        add(part, q * colour, full, c * half + q * colour, other, q * colour, colour)
        halve(q, 0)
    yield
    for step in range(4):
        size = colour >> (step + 1)
        for q in range(4):
            base = got_at[step] + q * size
            arrive(got, base, size, rsem.at[4 + 4 * step + q])
            add(part, offset[q], part, offset[q], got, base, size)
            if step < 3:
                halve(q, step + 1)
        if step < 3:
            yield
    last = colour >> 4
    for q in range(4):
        zin[q * last : (q + 1) * last, :] = part[rows(offset[q], last), :]
    piece = 4 * last // ZN
    for d in range(1, ZN):
        to = lax.rem(z + d, ZN)
        go(
            zin.at[rows(to * piece, piece)],
            zgot.at[pl.ds((d - 1) * piece, piece)],
            zs.at[d - 1],
            zr.at[d - 1],
            (to, g),
        )
    yield
    run = zin[rows(z * piece, piece), :].astype(F32)
    for d in range(1, ZN):
        arrive(zgot, (d - 1) * piece, piece, zr.at[d - 1])
        run = run + zgot[(d - 1) * piece : d * piece, :].astype(F32)
    zout[...] = run.astype(BF)
    for d in range(1, ZN):
        to = lax.rem(z + d, ZN)
        go(zout, zall.at[rows(z * piece, piece)], zs.at[6 + d], zr.at[6 + d], (to, g))
    zall[rows(z * piece, piece), :] = zout[...]
    yield
    for d in range(1, ZN):
        arrive(zall, 0, piece, zr.at[6 + d])
    for step in range(3, -1, -1):
        size = colour >> (step + 1)
        for q in range(4):
            if step == 3:
                gath[rows(offset[q], last), :] = zall[q * last : (q + 1) * last, :]
            else:
                axis, kind = STEPS[q][step + 1]
                arrive(gath, 0, size // 2, rsem.at[20 + 4 * (step + 1) + q])
                offset[q] = offset[q] - keep(axis, kind) * (size // 2)
            axis, kind = STEPS[q][step]
            sem = 20 + 4 * step + q
            here = gath.at[rows(offset[q], size)]
            go(here, here, ssem.at[sem], rsem.at[sem], partner(axis, kind))
        yield
    for q in range(4):
        arrive(gath, 0, colour // 2, rsem.at[20 + q])
        here = pl.ds(q * colour, colour)
        go(gath.at[here], back.at[here], ssem.at[36 + q], rsem.at[36 + q], twin)
    yield
    for q in range(4):
        arrive(back, q * colour, colour, rsem.at[36 + q])
        here = pl.ds(q * colour, colour)
        mine = (gath[here, :].astype(F32) * scale).astype(BF)
        theirs = (back[here, :].astype(F32) * scale).astype(BF)
        lanes = pl.ds(q * LANE, LANE)
        first = c == 0
        outs[0][layer, :, lanes] = jnp.where(first, mine, theirs)
        outs[1][layer, :, lanes] = jnp.where(first, theirs, mine)
    yield


def step_kernel(
    scale,
    col_ref,
    idx_ref,
    val_ref,
    feat_ref,
    cot_ref,
    ws_ref,
    wn_ref,
    self_ref,
    neigh_ref,
    in_ref,
    h,
    agg,
    pre,
    base,
    aggn,
    near,
    far,
    far_t,
    pick,
    pick_t,
    perm,
    out1,
    got1,
    out2,
    got2,
    full,
    part,
    other,
    got,
    gath,
    back,
    zin,
    zout,
    zgot,
    zall,
    s1,
    r1,
    s2,
    r2,
    ssem,
    rsem,
    zs,
    zr,
):
    z, g, x, y, c = place()
    node_rows, width = feat_ref.shape
    layers = ws_ref.shape[0]
    halo = idx_ref.shape[1]
    tile = val_ref.shape[2]
    wide = width // 2
    zrow, grow = halo // ZN, halo // GN

    def gpeer(d):
        px = lax.rem(x + d // 8, 4)
        py = lax.rem(y + lax.rem(d // 2, 4), 4)
        pc = lax.rem(c + lax.rem(d, 2), 2)
        return px * 8 + py * 2 + pc

    bar = pltpu.get_barrier_semaphore()
    for d in range(1, ZN):
        pl.semaphore_signal(
            bar, inc=1, device_id=(lax.rem(z + d, ZN), g), device_id_type=MESH
        )

    def greet(d, carry):
        pl.semaphore_signal(bar, inc=1, device_id=(z, gpeer(d)), device_id_type=MESH)
        return carry

    lax.fori_loop(1, GN, greet, 0)

    node = lax.broadcasted_iota(jnp.int32, (node_rows, halo), 0)
    pick_t[0] = (node == idx_ref[...]).astype(F32).astype(BF)
    pick[0] = pick_t[0].T
    i = lax.broadcasted_iota(jnp.int32, (halo, halo), 0)
    j = lax.broadcasted_iota(jnp.int32, (halo, halo), 1)
    perm[0] = (j == ((i >> 1) & 7) * 64 + (i >> 4) * 2 + (i & 1)).astype(F32).astype(BF)
    perm[1] = (j == ((i >> 1) & 31) * 16 + (i >> 6) * 2 + (i & 1)).astype(F32).astype(BF)
    pick[1] = dot(perm[0], pick[0]).astype(BF)
    tiles_near = node_rows // tile
    for r in range(col_ref.shape[0]):
        for t in range(tiles_near + halo // tile):
            block = jnp.zeros((tile, tile), F32)
            for b in range(col_ref.shape[1]):
                on = (col_ref[r, b] == t).astype(F32)
                block = block + val_ref[r, b].astype(F32) * on
            at = slice(r * tile, (r + 1) * tile)
            if t < tiles_near:
                near[at, t * tile : (t + 1) * tile] = block.astype(BF)
            else:
                k = t - tiles_near
                far[0, at, k * tile : (k + 1) * tile] = block.astype(BF)
    h[0] = feat_ref[...]
    pl.semaphore_wait(bar, ZN - 1 + GN - 1)

    def send_z(src, dst, s, r):
        for d in (4, 3, 5, 2, 6, 1, 7):
            to = lax.rem(z + d, ZN)
            copy(
                src.at[rows(to * zrow, zrow)], dst.at[rows(z * zrow, zrow)], s, r, (to, g)
            ).start()
        dst[rows(z * zrow, zrow), :] = src[rows(z * zrow, zrow), :]

    def send_g(src, dst, s, r):
        def body(d, carry):
            to = gpeer(d)
            copy(
                src.at[rows(to * grow, grow)], dst.at[rows(g * grow, grow)], s, r, (z, to)
            ).start()
            return carry

        lax.fori_loop(1, GN, body, 0)
        dst[rows(g * grow, grow), :] = src[rows(g * grow, grow), :]

    def wait_z(dst, r):
        here = dst.at[pl.ds(0, halo - zrow)]
        copy(here, here, r, r, (z, g)).wait_recv()

    def wait_g(dst, r):
        here = dst.at[pl.ds(0, halo - grow)]
        copy(here, here, r, r, (z, g)).wait_recv()

    def start(t, left, right):
        out1[t, 0] = left()
        send_z(out1.at[t, 0], got1.at[t, 0], s1.at[t, 0], r1.at[t, 0])
        out1[t, 1] = right()
        send_g(out1.at[t, 1], got1.at[t, 1], s1.at[t, 1], r1.at[t, 1])

    def turn_right(t):
        wait_g(got1.at[t, 1], r1.at[t, 1])
        out2[t, 1] = dot(perm[1], got1[t, 1]).astype(BF)
        send_z(out2.at[t, 1], got2.at[t, 1], s2.at[t, 1], r2.at[t, 1])

    def turn_left(t):
        wait_z(got1.at[t, 0], r1.at[t, 0])
        out2[t, 0] = dot(perm[0], got1[t, 0]).astype(BF)
        send_g(out2.at[t, 0], got2.at[t, 0], s2.at[t, 0], r2.at[t, 0])

    def forward(t, carry):
        start(
            t,
            lambda: dot(pick[0], h[t, :, :wide]).astype(BF),
            lambda: dot(pick[1], h[t, :, wide:]).astype(BF),
        )
        base[...] = dot(h[t], ws_ref[t])
        aggn[...] = dot(near[...], h[t])
        far[1] = dot(far[0], perm[1]).astype(BF)
        turn_right(t)
        turn_left(t)
        wait_g(got2.at[t, 0], r2.at[t, 0])
        agg[t, :, :wide] = (aggn[:, :wide] + dot(far[1], got2[t, 0])).astype(BF)
        wait_z(got2.at[t, 1], r2.at[t, 1])
        agg[t, :, wide:] = (aggn[:, wide:] + dot(far[0], got2[t, 1])).astype(BF)
        v = base[...] + dot(agg[t], wn_ref[t])
        pre[t] = v
        h[t + 1] = (v * jax.nn.sigmoid(v)).astype(BF)
        return carry

    lax.fori_loop(0, layers, forward, 0)
    for k in range(2):
        far_t[k] = far[k].T
    pick_t[1] = pick[1].T

    outs = (self_ref, neigh_ref)
    bufs = (full, part, other, got, gath, back, zin, zout, zgot, zall)
    sems = (ssem, rsem, zs, zr)
    sends, running = [], []

    def advance():
        for r in running:
            next(r)

    grad = cot_ref
    for at in range(layers - 1, -1, -1):
        t = 2 * layers - 1 - at
        v = pre[at]
        sigma = jax.nn.sigmoid(v)
        delta = (grad[...].astype(F32) * sigma * (1.0 + v * (1.0 - sigma))).astype(BF)
        up = dot(delta, wn_ref[at], AGAINST).astype(BF)
        start(
            t,
            lambda: dot(far_t[0], up[:, :wide]).astype(BF),
            lambda: dot(far_t[1], up[:, wide:]).astype(BF),
        )
        for m, left in enumerate((h, agg)):
            for k in range(2):
                term = dot(left[at], delta[:, k * wide : (k + 1) * wide], TRANSPOSED).astype(BF)
                for n in range(wide // LANE):
                    full[at, pl.ds((m * 4 + k * 2 + n) * width, width), :] = term[
                        :, n * LANE : (n + 1) * LANE
                    ]
        running.append(sum_stages(at, scale, outs, bufs, sems, sends))
        advance()
        base[...] = dot(delta, ws_ref[at], AGAINST) + dot(near[...], up, TRANSPOSED)
        turn_right(t)
        advance()
        turn_left(t)
        advance()
        wait_g(got2.at[t, 0], r2.at[t, 0])
        in_ref[:, :wide] = (base[:, :wide] + dot(pick_t[1], got2[t, 0])).astype(BF)
        wait_z(got2.at[t, 1], r2.at[t, 1])
        in_ref[:, wide:] = (base[:, wide:] + dot(pick_t[0], got2[t, 1])).astype(BF)
        grad = in_ref
    for run in running:
        pass
    alive = list(running)
    while alive:
        for run in list(alive):
            if next(run, "done") == "done":
                alive.remove(run)
    for move in sends:
        move.wait_send()

    def drain(t, carry):
        for k, (first, second) in enumerate(((zrow, grow), (grow, zrow))):
            for ref, sem, own in ((out1, s1, first), (out2, s2, second)):
                here = ref.at[t, k, pl.ds(0, halo - own)]
                copy(here, here, sem.at[t, k], sem.at[t, k], (z, g)).wait_send()
        return carry

    lax.fori_loop(0, 2 * layers, drain, 0)


def whole_step(col, idx, val, feat, cot, ws, wn, scale):
    layers, width, _ = ws.shape
    node_rows, halo = feat.shape[0], idx.shape[1]
    steps = 2 * layers
    total = 2 * width * width // LANE
    half = total // 2
    dma = pltpu.SemaphoreType.DMA
    vm = pltpu.VMEM

    def kernel(*refs):
        step_kernel(scale, *refs)

    grads = jax.ShapeDtypeStruct(ws.shape, BF)
    flow = vm((steps, 2, halo, width // 2), BF)
    return pl.pallas_call(
        kernel,
        out_shape=(grads, grads, jax.ShapeDtypeStruct(feat.shape, BF)),
        in_specs=[pl.BlockSpec(memory_space=pltpu.SMEM)]
        + [pl.BlockSpec(memory_space=pltpu.VMEM)] * 6,
        out_specs=[pl.BlockSpec(memory_space=pltpu.VMEM)] * 3,
        scratch_shapes=[
            vm((layers + 1, node_rows, width), BF),
            vm((layers, node_rows, width), BF),
            vm((layers, node_rows, width), F32),
            vm((node_rows, width), F32),
            vm((node_rows, width), F32),
            vm((node_rows, node_rows), BF),
            vm((2, node_rows, halo), BF),
            vm((2, halo, node_rows), BF),
            vm((2, halo, node_rows), BF),
            vm((2, node_rows, halo), BF),
            vm((2, halo, halo), BF),
            flow,
            flow,
            flow,
            flow,
            vm((layers, total, LANE), BF),
            vm((layers, half, LANE), BF),
            vm((layers, half, LANE), BF),
            vm((layers, half * 15 // 16, LANE), BF),
            vm((layers, half, LANE), BF),
            vm((layers, half, LANE), BF),
            vm((layers, half // 16, LANE), BF),
            vm((layers, half // 128, LANE), BF),
            vm((layers, half // 128 * 7, LANE), BF),
            vm((layers, half // 16, LANE), BF),
            dma((steps, 2)),
            dma((steps, 2)),
            dma((steps, 2)),
            dma((steps, 2)),
            dma((layers, 40)),
            dma((layers, 40)),
            dma((layers, 14)),
            dma((layers, 14)),
        ],
        compiler_params=pltpu.CompilerParams(
            collective_id=0, has_side_effects=True, vmem_limit_bytes=60 * 1024 * 1024
        ),
        name="whole_step",
    )(col, idx, val, feat, cot, ws, wn)


def per_device(
    features, cotangent, self_weight, neigh_weight, block_val, block_col, send_idx, send_count
):
    devices = lax.axis_size("gx") * lax.axis_size("gy")
    slots = send_idx.shape[2]
    scale = 1.0 / math.sqrt(features.shape[0] * devices)
    live = jnp.arange(slots, dtype=jnp.int32)[None, None, :] < send_count[:, :, None]
    idx = jnp.where(live, send_idx, -1).reshape(1, devices * slots)
    return whole_step(
        block_col, idx, block_val, features, cotangent, self_weight, neigh_weight, scale
    )


def solution(mesh):
    return jax.shard_map(
        per_device,
        mesh=mesh,
        in_specs=(
            P(("gx", "gy"), None),
            P(("gx", "gy"), None),
            P(),
            P(),
            P(("gx", "gy"), None, None, None),
            P(("gx", "gy"), None),
            P(("gx", "gy"), None, None),
            P(("gx", "gy"), None),
        ),
        out_specs=(P(), P(), P(("gx", "gy"), None)),
        check_vma=False,
    )
```

time: 508 us -> 160 us (0.31); the launches traced: 499 us -> 160 us
  waiting for transfers between devices: 329 us -> 0 us
  Pallas kernels: 0 us -> 153 us
  starting transfers between devices: 47.9 us -> 0 us
  local copies, waits for them, and re-layouts: 44.6 us -> 5.48 us
  matrix products: 34.4 us -> 0 us
  other arithmetic: 27.8 us -> 0.7 us
  between operations: 15.1 us -> 0.66 us
    psum x1 -> x0, waiting for transfers between devices: 224 us -> none  [packed_total(): so_far = lax.psum(vector, axis)]
    pallas_call x0 -> x1, Pallas kernels: none -> 153 us  [whole_step(): pl.pallas_call(kernel, out_shape=(grads, grads, jax.ShapeDtypeStruct(feat...]
    all_to_all x6 -> x0, waiting for transfers between devices: 105 us -> none  [exchange_both(): tiles = lax.all_to_all(tiles, axis, split_axis=0, concat_axis=0, tiled=True)]
    all_to_all x6 -> x0, starting transfers between devices: 47.9 us -> none  [exchange_both(): tiles = lax.all_to_all(tiles, axis, split_axis=0, concat_axis=0, tiled=True)]
    dot_general x27 -> x0, matrix products: 34.4 us -> none  [the longest x3 7.97 us: spread_back(): jnp.einsum('cn,njd->cjd', onehot, contrib.reshape(-1, tile, width), preci...]
    scatter-add x3 -> x0, other arithmetic: 12.3 us -> none  [per_device(): jnp.zeros((node_rows, width), jnp.float32).at[row_ids].add(masked)]
    another operation x12 -> x0, local copies, waits for them, and re-layouts: 11.8 us -> none  [the longest x3 4.62 us: per_device(): self_grad = jnp.stack(self_list)]
    gather x6 -> x0, local copies, waits for them, and re-layouts: 9.68 us -> none  [the longest x3 5.9 us: per_device(): jnp.take(hidden, row_ids, axis=0)]
  transfers between devices with their start and end apart: 7 -> 0, of which waited for: 7 -> 0; matrix products, arithmetic and copies ran while one was open for 5% -> 0% of each run, Pallas kernels for 0% -> 0%
where the time goes in v2:
time: 160 us
  Pallas kernels  153 us (96%)
  local copies, waits for them, and re-layouts  5.48 us (3%)
    pallas_call x1, Pallas kernels, whole_step(): pl.pallas_call(kernel, out_shape=(grads, grads, jax.ShapeDtypeStruct(feat...  153 us
    unnamed x7, local copies, waits for them, and re-layouts  4.62 us

profile of v2, /device:TPU:1, one launch (start us, length us, event | category | flops | bytes accessed | tf_op | source)
XLA Modules:
  0.0 159.6 jit_solution(13680063645959218997)
XLA Ops:
  0.6 0.7 compare_select_fusion
  1.3 0.1 copy.12
  1.5 0.7 reshape.48.refs_1_
  2.2 152.7 %whole_step.1 = (bf16[3,512,512]{2,1,0:T(8,128)(2,1)}, bf16[3,512,512]{2,1,0:T(8,128)(2,1)}, bf16[256,512]{1,0:T(8,128)(2,1)}) custom-call(s32[2,4]{1,0:T(2,128)} %refs_0_.1, s32[1,512]{1,0:T(1,128)} %reshape.48.refs_1_, bf16[2,4,128,128]{3,2,1,0:T(8,128)(2,1)} %refs_2_.1, bf16[256,512]{1,0:T(8,128)(2,1)} %refs_3_.1, bf16[256,512]{1,0:T(8,128)(2,1)} %refs_4_.1, ...), custom_call_target="tpu_custom_call" | custom-call | tf_op jit(solution)/shard_map/whole_step/pallas_call | solution.py:416
  154.9 0.0 copy-start
  154.9 2.8 %copy.16 = bf16[3,512,512]{2,1,0:T(8,128)(2,1)} copy(bf16[3,512,512]{2,1,0:T(8,128)(2,1)} %get-tuple-element.6) | data formatting | bytes 3145728
  157.7 0.0 copy-done
  157.7 0.0 copy-start.1
  157.7 1.1 copy.17
  158.9 0.0 copy-done.1
  158.9 0.7 copy.18
Async XLA Ops:
  154.9 2.8 %copy-start = (bf16[3,512,512]{2,1,0:T(8,128)(2,1)S(1)}, bf16[3,512,512]{2,1,0:T(8,128)(2,1)}, u32[]{:S(2)}) copy-start(bf16[3,512,512]{2,1,0:T(8,128)(2,1)} %get-tuple-element.7) | copy-start | bytes 4718596
  157.7 1.1 copy-start.1

commit v3 on v2

v3 whole, which is shorter than its diff:
```python
import math

import jax
import jax.numpy as jnp
from jax import lax
from jax.experimental import pallas as pl
from jax.experimental.pallas import tpu as pltpu
from jax.sharding import PartitionSpec as P

MESH = pl.DeviceIdType.MESH
LANE = 128
BF, F32 = jnp.bfloat16, jnp.float32
ROWS = (((1,), (0,)), ((), ()))
TRANSPOSED = (((0,), (0,)), ((), ()))
AGAINST = (((1,), (1,)), ((), ()))


def dot(a, b, dims=ROWS):
    return lax.dot_general(a, b, dims, preferred_element_type=F32)


def place():
    z, g = lax.axis_index("gx"), lax.axis_index("gy")
    x, y, c = g // 8, lax.rem(g // 2, 4), lax.rem(g, 2)
    return z, g, x, y, c


def rows(start, size):
    return pl.ds(pl.multiple_of(start, 16), size)


def copy(src, dst, s, r, peer):
    return pltpu.make_async_remote_copy(
        src_ref=src, dst_ref=dst, send_sem=s, recv_sem=r, device_id=peer, device_id_type=MESH
    )


ZN, GN = 8, 32


def sum_stages(layer, outs, bufs, sems, sends):
    z, g, x, y, c = place()
    full, part, other, got, gath, back, zin, zout, zgot, zall = (b.at[layer] for b in bufs)
    ssem, rsem, zs, zr = (s.at[layer] for s in sems)
    half = part.shape[0]
    colour = half // 2
    first, second = colour // 4, colour // 16
    twin = (z, x * 8 + y * 2 + 1 - c)
    axes = ((x, 8, y * 2 + c), (y, 2, x * 8 + c))

    def go(*args):
        move = copy(*args)
        move.start()
        sends.append(move)

    def arrive(ref, start, size, sem):
        here = ref.at[pl.ds(start, size)]
        copy(here, here, zs.at[0], sem, twin).wait_recv()

    def ring(axis, d):
        p, stride, rest = axes[axis]
        to = lax.rem(p + d, 4)
        return to, (z, to * stride + rest)

    def scatter(q, axis, base, size, land, sem):
        for d in range(1, 4):
            to, peer = ring(axis, d)
            go(
                part.at[rows(base + to * size, size)],
                got.at[pl.ds(land + (d - 1) * size, size)],
                ssem.at[sem + d - 1],
                rsem.at[sem + d - 1],
                peer,
            )

    def collect(base, size, land, sem):
        run = part[rows(base, size), :].astype(F32)
        for d in range(3):
            arrive(got, land + d * size, size, rsem.at[sem + d])
            run = run + got[land + d * size : land + (d + 1) * size, :].astype(F32)
        return run.astype(BF)

    def spread(axis, base, size, sem):
        for d in range(1, 4):
            here = gath.at[rows(base, size)]
            go(here, here, ssem.at[sem + d - 1], rsem.at[sem + d - 1], ring(axis, d)[1])

    for q in range(2):
        src = full.at[rows((1 - c) * half + q * colour, colour)]
        go(src, other.at[pl.ds(q * colour, colour)], ssem.at[q], rsem.at[q], twin)
    yield
    outer, inner = [], []
    for q in range(2):
        arrive(other, q * colour, colour, rsem.at[q])
        for k in range(4):
            at = q * colour + k * first
            s = full[rows(c * half + at, first), :].astype(F32)
            part[at : at + first, :] = (s + other[at : at + first, :].astype(F32)).astype(BF)
        scatter(q, q, q * colour, first, q * 3 * first, 2 + 3 * q)
        outer.append(q * colour + axes[q][0] * first)
        inner.append(outer[q] + axes[1 - q][0] * second)
    yield
    for q in range(2):
        part[rows(outer[q], first), :] = collect(outer[q], first, q * 3 * first, 2 + 3 * q)
        scatter(q, 1 - q, outer[q], second, 6 * first + q * 3 * second, 8 + 3 * q)
    yield
    for q in range(2):
        zin[q * second : (q + 1) * second, :] = collect(
            inner[q], second, 6 * first + q * 3 * second, 8 + 3 * q
        )
    piece = 2 * second // ZN
    for d in range(1, ZN):
        to = lax.rem(z + d, ZN)
        go(
            zin.at[rows(to * piece, piece)],
            zgot.at[pl.ds((d - 1) * piece, piece)],
            zs.at[d - 1],
            zr.at[d - 1],
            (to, g),
        )
    yield
    run = zin[rows(z * piece, piece), :].astype(F32)
    for d in range(1, ZN):
        arrive(zgot, (d - 1) * piece, piece, zr.at[d - 1])
        run = run + zgot[(d - 1) * piece : d * piece, :].astype(F32)
    zout[...] = run.astype(BF)
    for d in range(1, ZN):
        to = lax.rem(z + d, ZN)
        go(zout, zall.at[rows(z * piece, piece)], zs.at[6 + d], zr.at[6 + d], (to, g))
    zall[rows(z * piece, piece), :] = zout[...]
    yield
    for d in range(1, ZN):
        arrive(zall, 0, piece, zr.at[6 + d])
    for q in range(2):
        gath[rows(inner[q], second), :] = zall[q * second : (q + 1) * second, :]
        spread(1 - q, inner[q], second, 14 + 3 * q)
    yield
    for q in range(2):
        for d in range(3):
            arrive(gath, 0, second, rsem.at[14 + 3 * q + d])
        spread(q, outer[q], first, 20 + 3 * q)
    yield
    for q in range(2):
        for d in range(3):
            arrive(gath, 0, first, rsem.at[20 + 3 * q + d])
        here = pl.ds(q * colour, colour)
        go(gath.at[here], back.at[here], ssem.at[26 + q], rsem.at[26 + q], twin)
    yield
    width = outs[0].shape[1]
    for k in range(half // width):
        if k % 2 == 0:
            arrive(back, (k // 2) * colour, colour, rsem.at[26 + k // 2])
        here = pl.ds(k * width, width)
        mine, theirs = gath[here, :], back[here, :]
        lanes = pl.ds(k * LANE, LANE)
        even = c == 0
        outs[0][layer, :, lanes] = jnp.where(even, mine, theirs)
        outs[1][layer, :, lanes] = jnp.where(even, theirs, mine)
    yield


def step_kernel(
    col_in,
    idx_in,
    cnt_in,
    val_in,
    feat_in,
    cot_in,
    ws_in,
    wn_in,
    self_ref,
    neigh_ref,
    in_ref,
    col_ref,
    idx_ref,
    cnt_ref,
    val_ref,
    cot_ref,
    ws_ref,
    wn_ref,
    h,
    agg,
    pre,
    base,
    aggn,
    near,
    far,
    far_t,
    pick,
    pick_t,
    perm,
    out1,
    got1,
    out2,
    got2,
    full,
    part,
    other,
    got,
    gath,
    back,
    zin,
    zout,
    zgot,
    zall,
    s1,
    r1,
    s2,
    r2,
    ssem,
    rsem,
    zs,
    zr,
    load,
):
    z, g, x, y, c = place()
    node_rows, width = feat_in.shape
    layers = ws_in.shape[0]
    devices = idx_in.shape[1]
    halo = devices * idx_in.shape[0]
    tile = val_ref.shape[2]
    wide = width // 2
    zrow, grow = halo // ZN, halo // GN

    def gpeer(d):
        px = lax.rem(x + d // 8, 4)
        py = lax.rem(y + lax.rem(d // 2, 4), 4)
        pc = lax.rem(c + lax.rem(d, 2), 2)
        return px * 8 + py * 2 + pc

    loads = [
        pltpu.make_async_copy(src, dst, load.at[k])
        for k, (src, dst) in enumerate(
            (
                (idx_in, idx_ref),
                (cnt_in, cnt_ref),
                (feat_in, h.at[0]),
                (val_in, val_ref),
                (col_in, col_ref),
                (ws_in, ws_ref),
                (wn_in, wn_ref),
                (cot_in, cot_ref),
            )
        )
    ]
    for move in loads:
        move.start()
    bar = pltpu.get_barrier_semaphore()
    for d in range(1, ZN):
        pl.semaphore_signal(
            bar, inc=1, device_id=(lax.rem(z + d, ZN), g), device_id_type=MESH
        )

    def greet(d, carry):
        pl.semaphore_signal(bar, inc=1, device_id=(z, gpeer(d)), device_id_type=MESH)
        return carry

    lax.fori_loop(1, GN, greet, 0)

    i = lax.broadcasted_iota(jnp.int32, (halo, halo), 0)
    j = lax.broadcasted_iota(jnp.int32, (halo, halo), 1)

    def one_hot(target):
        return (j == target).astype(F32).astype(BF)

    node = lax.broadcasted_iota(jnp.int32, (node_rows, devices), 0)
    loads[0].wait()
    loads[1].wait()
    for s in range(halo // devices):
        row = jnp.where(s < cnt_ref[...], idx_ref[s : s + 1, :], -1)
        pick_t[0, :, s * devices : (s + 1) * devices] = (node == row).astype(F32).astype(BF)
    pick[0] = pick_t[0].T
    by_slot = pick[0]
    pick[1] = dot(one_hot((i & 1) * 256 + ((i >> 1) & 7) * 32 + (i >> 4)), by_slot).astype(BF)
    pick[0] = dot(one_hot((i & 1) * 256 + (i >> 1)), by_slot).astype(BF)
    loads[2].wait()

    def constants():
        perm[0] = one_hot(((i >> 1) & 7) * 64 + (i >> 4) * 2 + (i & 1))
        perm[1] = one_hot(((i >> 1) & 31) * 16 + (i >> 6) * 2 + (i & 1))
        for move in loads[3:]:
            move.wait()
        tiles_near = node_rows // tile
        for r in range(col_ref.shape[0]):
            for t in range(tiles_near + halo // tile):
                block = jnp.zeros((tile, tile), F32)
                for b in range(col_ref.shape[1]):
                    on = (col_ref[r, b] == t).astype(F32)
                    block = block + val_ref[r, b].astype(F32) * on
                at = slice(r * tile, (r + 1) * tile)
                if t < tiles_near:
                    near[at, t * tile : (t + 1) * tile] = block.astype(BF)
                else:
                    k = t - tiles_near
                    far[0, at, k * tile : (k + 1) * tile] = block.astype(BF)
        far[1] = dot(far[0], perm[1]).astype(BF)

    pl.semaphore_wait(bar, ZN - 1 + GN - 1)

    def send_z(src, dst, s, r):
        for d in (4, 3, 5, 2, 6, 1, 7):
            to = lax.rem(z + d, ZN)
            copy(
                src.at[rows(to * zrow, zrow)], dst.at[rows(z * zrow, zrow)], s, r, (to, g)
            ).start()
        dst[rows(z * zrow, zrow), :] = src[rows(z * zrow, zrow), :]

    def send_g(src, dst, s, r):
        def body(d, carry):
            to = gpeer(d)
            copy(
                src.at[rows(to * grow, grow)], dst.at[rows(g * grow, grow)], s, r, (z, to)
            ).start()
            return carry

        lax.fori_loop(1, GN, body, 0)
        dst[rows(g * grow, grow), :] = src[rows(g * grow, grow), :]

    def wait_z(dst, r):
        here = dst.at[pl.ds(0, halo - zrow)]
        copy(here, here, r, r, (z, g)).wait_recv()

    def wait_g(dst, r):
        here = dst.at[pl.ds(0, halo - grow)]
        copy(here, here, r, r, (z, g)).wait_recv()

    def start(t, left, right):
        out1[t, 1] = right()
        send_g(out1.at[t, 1], got1.at[t, 1], s1.at[t, 1], r1.at[t, 1])
        out1[t, 0] = left()
        send_z(out1.at[t, 0], got1.at[t, 0], s1.at[t, 0], r1.at[t, 0])

    def turn_right(t):
        wait_g(got1.at[t, 1], r1.at[t, 1])
        out2[t, 1] = dot(perm[1], got1[t, 1]).astype(BF)
        send_z(out2.at[t, 1], got2.at[t, 1], s2.at[t, 1], r2.at[t, 1])

    def turn_left(t):
        wait_z(got1.at[t, 0], r1.at[t, 0])
        out2[t, 0] = dot(perm[0], got1[t, 0]).astype(BF)
        send_g(out2.at[t, 0], got2.at[t, 0], s2.at[t, 0], r2.at[t, 0])

    def slope(v):
        sigma = jax.nn.sigmoid(v)
        return sigma * (1.0 + v * (1.0 - sigma))

    def forward(t, between):
        start(
            t,
            lambda: dot(pick[0], h[t, :, :wide]).astype(BF),
            lambda: dot(pick[1], h[t, :, wide:]).astype(BF),
        )
        between()
        base[...] = dot(h[t], ws_ref[t])
        aggn[...] = dot(near[...], h[t])
        turn_right(t)
        turn_left(t)
        wait_g(got2.at[t, 0], r2.at[t, 0])
        agg[t, :, :wide] = (aggn[:, :wide] + dot(far[1], got2[t, 0])).astype(BF)
        base[...] += dot(agg[t, :, :wide], wn_ref[t, :wide, :])
        wait_z(got2.at[t, 1], r2.at[t, 1])
        agg[t, :, wide:] = (aggn[:, wide:] + dot(far[0], got2[t, 1])).astype(BF)
        v = base[...] + dot(agg[t, :, wide:], wn_ref[t, wide:, :])
        pre[t] = v
        h[t + 1] = (v * jax.nn.sigmoid(v)).astype(BF)

    forward(0, constants)

    def later(t, carry):
        def between():
            pre[t - 1] = slope(pre[t - 1])

        forward(t, between)
        return carry

    lax.fori_loop(1, layers, later, 0)
    for k in range(2):
        far_t[k] = far[k].T
        pick_t[k] = pick[k].T

    outs = (self_ref, neigh_ref)
    bufs = (full, part, other, got, gath, back, zin, zout, zgot, zall)
    sems = (ssem, rsem, zs, zr)
    sends, running = [], []

    def advance():
        for run in list(running):
            if next(run, "done") == "done":
                running.remove(run)

    grad = cot_ref
    for at in range(layers - 1, -1, -1):
        t = 2 * layers - 1 - at
        if at == layers - 1:
            pre[at] = slope(pre[at])
        delta = (grad[...].astype(F32) * pre[at]).astype(BF)
        up = dot(delta, wn_ref[at], AGAINST).astype(BF)
        start(
            t,
            lambda: dot(far_t[0], up[:, :wide]).astype(BF),
            lambda: dot(far_t[1], up[:, wide:]).astype(BF),
        )
        for m, left in enumerate((h, agg)):
            for k in range(2):
                term = dot(left[at], delta[:, k * wide : (k + 1) * wide], TRANSPOSED).astype(BF)
                for n in range(wide // LANE):
                    full[at, pl.ds((m * 4 + k * 2 + n) * width, width), :] = term[
                        :, n * LANE : (n + 1) * LANE
                    ]
        running.append(sum_stages(at, outs, bufs, sems, sends))
        advance()
        base[...] = dot(delta, ws_ref[at], AGAINST) + dot(near[...], up, TRANSPOSED)
        advance()
        turn_right(t)
        advance()
        turn_left(t)
        advance()
        wait_g(got2.at[t, 0], r2.at[t, 0])
        in_ref[:, :wide] = (base[:, :wide] + dot(pick_t[1], got2[t, 0])).astype(BF)
        advance()
        wait_z(got2.at[t, 1], r2.at[t, 1])
        in_ref[:, wide:] = (base[:, wide:] + dot(pick_t[0], got2[t, 1])).astype(BF)
        grad = in_ref
    while running:
        advance()
    for move in sends:
        move.wait_send()

    def drain(t, carry):
        for k, (first, second) in enumerate(((zrow, grow), (grow, zrow))):
            for ref, sem, own in ((out1, s1, first), (out2, s2, second)):
                here = ref.at[t, k, pl.ds(0, halo - own)]
                copy(here, here, sem.at[t, k], sem.at[t, k], (z, g)).wait_send()
        return carry

    lax.fori_loop(0, 2 * layers, drain, 0)


def whole_step(col, idx, cnt, val, feat, cot, ws, wn):
    layers, width, _ = ws.shape
    node_rows, halo = feat.shape[0], idx.shape[0] * idx.shape[1]
    steps = 2 * layers
    total = 2 * width * width // LANE
    half = total // 2
    dma = pltpu.SemaphoreType.DMA
    vm = pltpu.VMEM

    grads = jax.ShapeDtypeStruct(ws.shape, BF)
    flow = vm((steps, 2, halo, width // 2), BF)
    return pl.pallas_call(
        step_kernel,
        out_shape=(grads, grads, jax.ShapeDtypeStruct(feat.shape, BF)),
        in_specs=[pl.BlockSpec(memory_space=pltpu.HBM)] * 8,
        out_specs=[pl.BlockSpec(memory_space=pltpu.VMEM)] * 3,
        scratch_shapes=[
            pltpu.SMEM(col.shape, col.dtype),
            vm(idx.shape, idx.dtype),
            vm(cnt.shape, cnt.dtype),
            vm(val.shape, BF),
            vm(cot.shape, BF),
            vm(ws.shape, BF),
            vm(wn.shape, BF),
            vm((layers + 1, node_rows, width), BF),
            vm((layers, node_rows, width), BF),
            vm((layers, node_rows, width), F32),
            vm((node_rows, width), F32),
            vm((node_rows, width), F32),
            vm((node_rows, node_rows), BF),
            vm((2, node_rows, halo), BF),
            vm((2, halo, node_rows), BF),
            vm((2, halo, node_rows), BF),
            vm((2, node_rows, halo), BF),
            vm((2, halo, halo), BF),
            flow,
            flow,
            flow,
            flow,
            vm((layers, total, LANE), BF),
            vm((layers, half, LANE), BF),
            vm((layers, half, LANE), BF),
            vm((layers, half * 15 // 16, LANE), BF),
            vm((layers, half, LANE), BF),
            vm((layers, half, LANE), BF),
            vm((layers, half // 16, LANE), BF),
            vm((layers, half // 128, LANE), BF),
            vm((layers, half // 128 * 7, LANE), BF),
            vm((layers, half // 16, LANE), BF),
            dma((steps, 2)),
            dma((steps, 2)),
            dma((steps, 2)),
            dma((steps, 2)),
            dma((layers, 28)),
            dma((layers, 28)),
            dma((layers, 14)),
            dma((layers, 14)),
            dma((8,)),
        ],
        compiler_params=pltpu.CompilerParams(
            collective_id=0, has_side_effects=True, vmem_limit_bytes=60 * 1024 * 1024
        ),
        name="whole_step",
    )(col, idx, cnt, val, feat, cot, ws, wn)


def per_device(
    features, cotangent, self_weight, neigh_weight, block_val, block_col, send_idx, send_count
):
    devices = lax.axis_size("gx") * lax.axis_size("gy")
    slots = send_idx.shape[2]
    scale = 1.0 / math.sqrt(features.shape[0] * devices)
    self_sum, neigh_sum, grad = whole_step(
        block_col,
        send_idx.reshape(devices, slots).T,
        send_count,
        block_val,
        features,
        cotangent,
        self_weight,
        neigh_weight,
    )

    def scaled(total):
        return (total.astype(F32) * scale).astype(BF)

    return scaled(self_sum), scaled(neigh_sum), grad


def solution(mesh):
    return jax.shard_map(
        per_device,
        mesh=mesh,
        in_specs=(
            P(("gx", "gy"), None),
            P(("gx", "gy"), None),
            P(),
            P(),
            P(("gx", "gy"), None, None, None),
            P(("gx", "gy"), None),
            P(("gx", "gy"), None, None),
            P(("gx", "gy"), None),
        ),
        out_specs=(P(), P(), P(("gx", "gy"), None)),
        check_vma=False,
    )
```

time: 160 us -> 160 us (level)
  local copies, waits for them, and re-layouts: 5.48 us -> 0.71 us
  other arithmetic: 0.7 us -> 4.21 us
  Pallas kernels: 153 us -> 155 us
    convert_element_type x0 -> x1, other arithmetic: none -> 4.21 us  [scaled(): return (total.astype(F32) * scale).astype(BF)]
    unnamed x7 -> x3, local copies, waits for them, and re-layouts: 4.62 us -> 0.71 us
    pallas_call x1, Pallas kernels: 153 us -> 155 us  [whole_step(): pl.pallas_call(step_kernel, out_shape=(grads, grads, jax.ShapeDtypeStruct...]
where the time goes in v3:
time: 160 us
  Pallas kernels  155 us (97%)
  other arithmetic  4.21 us (3%)
    pallas_call x1, Pallas kernels, whole_step(): pl.pallas_call(step_kernel, out_shape=(grads, grads, jax.ShapeDtypeStruct...  155 us
    convert_element_type x1, other arithmetic, scaled(): return (total.astype(F32) * scale).astype(BF)  4.21 us

profile of v3, /device:TPU:1, one launch (start us, length us, event | category | flops | bytes accessed | tf_op | source)
XLA Modules:
  0.0 160.1 jit_solution(3610375925312947827)
XLA Ops:
  0.6 154.6 %whole_step.1 = (bf16[3,512,512]{2,1,0:T(8,128)(2,1)}, bf16[3,512,512]{2,1,0:T(8,128)(2,1)}, bf16[256,512]{1,0:T(8,128)(2,1)}) custom-call(s32[2,4]{1,0:T(2,128)} %col_in.1, s32[2,256]{1,0:T(2,128)} %bitcast.3, s32[1,256]{1,0:T(1,128)} %cnt_in.1, bf16[2,4,128,128]{3,2,1,0:T(8,128)(2,1)} %val_in.1, bf16[256,512]{1,0:T(8,128)(2,1)} %feat_in.1, ...), custom_call_target="tpu_custom_call" | custom-call | tf_op jit(solution)/shard_map/whole_step/pallas_call | solution.py:450
  155.2 0.0 copy-start
  155.2 4.2 %multiply_convert_fusion = (bf16[3,512,512]{2,1,0:T(8,128)(2,1)}, bf16[3,512,512]{2,1,0:T(8,128)(2,1)}) fusion(bf16[3,512,512]{2,1,0:T(8,128)(2,1)} %get-tuple-element.7, bf16[3,512,512]{2,1,0:T(8,128)(2,1)} %get-tuple-element.6), kind=kLoop, calls=%fused_computation | loop fusion | flops 4718592 | bytes 6291456 | tf_op jit(solution)/shard_map/convert_element_type | solution.py:523
  159.4 0.0 copy-done
  159.4 0.7 copy.12
Async XLA Ops:
  155.2 4.2 %copy-start = (bf16[256,512]{1,0:T(8,128)(2,1)S(1)}, bf16[256,512]{1,0:T(8,128)(2,1)}, u32[]{:S(2)}) copy-start(bf16[256,512]{1,0:T(8,128)(2,1)} %get-tuple-element.16) | copy-start | bytes 786436

commit v4 on v3

--- a/solution.py
+++ b/solution.py
@@ -88,7 +88,7 @@
     for q in range(2):
         src = full.at[rows((1 - c) * half + q * colour, colour)]
         go(src, other.at[pl.ds(q * colour, colour)], ssem.at[q], rsem.at[q], twin)
-    yield
+    yield True
     outer, inner = [], []
     for q in range(2):
         arrive(other, q * colour, colour, rsem.at[q])
@@ -99,11 +99,11 @@
         scatter(q, q, q * colour, first, q * 3 * first, 2 + 3 * q)
         outer.append(q * colour + axes[q][0] * first)
         inner.append(outer[q] + axes[1 - q][0] * second)
-    yield
+    yield False
     for q in range(2):
         part[rows(outer[q], first), :] = collect(outer[q], first, q * 3 * first, 2 + 3 * q)
         scatter(q, 1 - q, outer[q], second, 6 * first + q * 3 * second, 8 + 3 * q)
-    yield
+    yield False
     for q in range(2):
         zin[q * second : (q + 1) * second, :] = collect(
             inner[q], second, 6 * first + q * 3 * second, 8 + 3 * q
@@ -118,7 +118,7 @@
             zr.at[d - 1],
             (to, g),
         )
-    yield
+    yield False
     run = zin[rows(z * piece, piece), :].astype(F32)
     for d in range(1, ZN):
         arrive(zgot, (d - 1) * piece, piece, zr.at[d - 1])
@@ -128,24 +128,24 @@
         to = lax.rem(z + d, ZN)
         go(zout, zall.at[rows(z * piece, piece)], zs.at[6 + d], zr.at[6 + d], (to, g))
     zall[rows(z * piece, piece), :] = zout[...]
-    yield
+    yield False
     for d in range(1, ZN):
         arrive(zall, 0, piece, zr.at[6 + d])
     for q in range(2):
         gath[rows(inner[q], second), :] = zall[q * second : (q + 1) * second, :]
         spread(1 - q, inner[q], second, 14 + 3 * q)
-    yield
+    yield True
     for q in range(2):
         for d in range(3):
             arrive(gath, 0, second, rsem.at[14 + 3 * q + d])
         spread(q, outer[q], first, 20 + 3 * q)
-    yield
+    yield False
     for q in range(2):
         for d in range(3):
             arrive(gath, 0, first, rsem.at[20 + 3 * q + d])
         here = pl.ds(q * colour, colour)
         go(gath.at[here], back.at[here], ssem.at[26 + q], rsem.at[26 + q], twin)
-    yield
+    yield False
     width = outs[0].shape[1]
     for k in range(half // width):
         if k % 2 == 0:
@@ -156,7 +156,7 @@
         even = c == 0
         outs[0][layer, :, lanes] = jnp.where(even, mine, theirs)
         outs[1][layer, :, lanes] = jnp.where(even, theirs, mine)
-    yield
+    yield False
 
 
 def step_kernel(
@@ -305,15 +305,26 @@
             ).start()
         dst[rows(z * zrow, zrow), :] = src[rows(z * zrow, zrow), :]
 
+    ys = [lax.rem(y + d, 4) for d in range(4)]
+    cs = [c, 1 - c]
+
     def send_g(src, dst, s, r):
+        def part(px, own):
+            for dy in (2, 1, 3, 0):
+                for dc in (1, 0):
+                    if own and dy == 0 and dc == 0:
+                        continue
+                    to = px * 8 + ys[dy] * 2 + cs[dc]
+                    copy(
+                        src.at[rows(to * grow, grow)], dst.at[rows(g * grow, grow)], s, r, (z, to)
+                    ).start()
+
         def body(d, carry):
-            to = gpeer(d)
-            copy(
-                src.at[rows(to * grow, grow)], dst.at[rows(g * grow, grow)], s, r, (z, to)
-            ).start()
+            part(lax.rem(x + d, 4), False)
             return carry
 
-        lax.fori_loop(1, GN, body, 0)
+        lax.fori_loop(1, 4, body, 0)
+        part(x, True)
         dst[rows(g * grow, grow), :] = src[rows(g * grow, grow), :]
 
     def wait_z(dst, r):
@@ -325,10 +336,10 @@
         copy(here, here, r, r, (z, g)).wait_recv()
 
     def start(t, left, right):
+        out1[t, 0] = left()
+        send_z(out1.at[t, 0], got1.at[t, 0], s1.at[t, 0], r1.at[t, 0])
         out1[t, 1] = right()
         send_g(out1.at[t, 1], got1.at[t, 1], s1.at[t, 1], r1.at[t, 1])
-        out1[t, 0] = left()
-        send_z(out1.at[t, 0], got1.at[t, 0], s1.at[t, 0], r1.at[t, 0])
 
     def turn_right(t):
         wait_g(got1.at[t, 1], r1.at[t, 1])
@@ -383,10 +394,14 @@
     sems = (ssem, rsem, zs, zr)
     sends, running = [], []
 
-    def advance():
-        for run in list(running):
-            if next(run, "done") == "done":
-                running.remove(run)
+    def advance(much=True, only=None):
+        for entry in list(running):
+            run, layer, heavy = entry
+            if (heavy and not much) or only not in (None, layer):
+                continue
+            entry[2] = next(run, None)
+            if entry[2] is None:
+                running.remove(entry)
 
     grad = cot_ref
     for at in range(layers - 1, -1, -1):
@@ -407,17 +422,19 @@
                     full[at, pl.ds((m * 4 + k * 2 + n) * width, width), :] = term[
                         :, n * LANE : (n + 1) * LANE
                     ]
-        running.append(sum_stages(at, outs, bufs, sems, sends))
+        running.append([sum_stages(at, outs, bufs, sems, sends), at, False])
         advance()
         base[...] = dot(delta, ws_ref[at], AGAINST) + dot(near[...], up, TRANSPOSED)
-        advance()
+        if at == 0:
+            advance()
         turn_right(t)
-        advance()
         turn_left(t)
-        advance()
+        advance(much=False)
+        advance(much=False)
         wait_g(got2.at[t, 0], r2.at[t, 0])
         in_ref[:, :wide] = (base[:, :wide] + dot(pick_t[1], got2[t, 0])).astype(BF)
-        advance()
+        if at == 0:
+            advance(only=0)
         wait_z(got2.at[t, 1], r2.at[t, 1])
         in_ref[:, wide:] = (base[:, wide:] + dot(pick_t[0], got2[t, 1])).astype(BF)
         grad = in_ref

time: 160 us -> 143 us (0.89)
  Pallas kernels: 155 us -> 138 us
    pallas_call x1, Pallas kernels: 155 us -> 138 us  [whole_step(): pl.pallas_call(step_kernel, out_shape=(grads, grads, jax.ShapeDtypeStruct...]
where the time goes in v4:
time: 143 us
  Pallas kernels  138 us (97%)
  other arithmetic  4.21 us (3%)
    pallas_call x1, Pallas kernels, whole_step(): pl.pallas_call(step_kernel, out_shape=(grads, grads, jax.ShapeDtypeStruct...  138 us
    convert_element_type x1, other arithmetic, scaled(): return (total.astype(F32) * scale).astype(BF)  4.21 us

profile of v4, /device:TPU:1, one launch (start us, length us, event | category | flops | bytes accessed | tf_op | source)
XLA Modules:
  0.0 143.1 jit_solution(16189939235796476012)
XLA Ops:
  0.6 137.5 %whole_step.1 = (bf16[3,512,512]{2,1,0:T(8,128)(2,1)}, bf16[3,512,512]{2,1,0:T(8,128)(2,1)}, bf16[256,512]{1,0:T(8,128)(2,1)}) custom-call(s32[2,4]{1,0:T(2,128)} %col_in.1, s32[2,256]{1,0:T(2,128)} %bitcast.3, s32[1,256]{1,0:T(1,128)} %cnt_in.1, bf16[2,4,128,128]{3,2,1,0:T(8,128)(2,1)} %val_in.1, bf16[256,512]{1,0:T(8,128)(2,1)} %feat_in.1, ...), custom_call_target="tpu_custom_call" | custom-call | tf_op jit(solution)/shard_map/whole_step/pallas_call | solution.py:467
  138.1 0.0 copy-start
  138.2 4.2 %multiply_convert_fusion = (bf16[3,512,512]{2,1,0:T(8,128)(2,1)}, bf16[3,512,512]{2,1,0:T(8,128)(2,1)}) fusion(bf16[3,512,512]{2,1,0:T(8,128)(2,1)} %get-tuple-element.7, bf16[3,512,512]{2,1,0:T(8,128)(2,1)} %get-tuple-element.6), kind=kLoop, calls=%fused_computation | loop fusion | flops 4718592 | bytes 6291456 | tf_op jit(solution)/shard_map/convert_element_type | solution.py:540
  142.4 0.0 copy-done
  142.4 0.7 copy.12
Async XLA Ops:
  138.1 4.2 %copy-start = (bf16[256,512]{1,0:T(8,128)(2,1)S(1)}, bf16[256,512]{1,0:T(8,128)(2,1)}, u32[]{:S(2)}) copy-start(bf16[256,512]{1,0:T(8,128)(2,1)} %get-tuple-element.16) | copy-start | bytes 786436

commit v5 on v4

--- a/solution.py
+++ b/solution.py
@@ -222,11 +222,8 @@
     wide = width // 2
     zrow, grow = halo // ZN, halo // GN
 
-    def gpeer(d):
-        px = lax.rem(x + d // 8, 4)
-        py = lax.rem(y + lax.rem(d // 2, 4), 4)
-        pc = lax.rem(c + lax.rem(d, 2), 2)
-        return px * 8 + py * 2 + pc
+    ys = [lax.rem(y + d, 4) for d in range(4)]
+    cs = [c, 1 - c]
 
     loads = [
         pltpu.make_async_copy(src, dst, load.at[k])
@@ -251,11 +248,19 @@
             bar, inc=1, device_id=(lax.rem(z + d, ZN), g), device_id_type=MESH
         )
 
-    def greet(d, carry):
-        pl.semaphore_signal(bar, inc=1, device_id=(z, gpeer(d)), device_id_type=MESH)
+    def greet(px, own):
+        for dy in range(4):
+            for dc in range(2):
+                if not (own and dy == 0 and dc == 0):
+                    peer = (z, px * 8 + ys[dy] * 2 + cs[dc])
+                    pl.semaphore_signal(bar, inc=1, device_id=peer, device_id_type=MESH)
+
+    def greet_far(d, carry):
+        greet(lax.rem(x + d, 4), False)
         return carry
 
-    lax.fori_loop(1, GN, greet, 0)
+    lax.fori_loop(1, 4, greet_far, 0)
+    greet(x, True)
 
     i = lax.broadcasted_iota(jnp.int32, (halo, halo), 0)
     j = lax.broadcasted_iota(jnp.int32, (halo, halo), 1)
@@ -305,9 +310,6 @@
             ).start()
         dst[rows(z * zrow, zrow), :] = src[rows(z * zrow, zrow), :]
 
-    ys = [lax.rem(y + d, 4) for d in range(4)]
-    cs = [c, 1 - c]
-
     def send_g(src, dst, s, r):
         def part(px, own):
             for dy in (2, 1, 3, 0):
@@ -395,7 +397,7 @@
     sends, running = [], []
 
     def advance(much=True, only=None):
-        for entry in list(running):
+        for entry in reversed(list(running)):
             run, layer, heavy = entry
             if (heavy and not much) or only not in (None, layer):
                 continue

time: 143 us -> 139 us (0.972)
  Pallas kernels: 138 us -> 133 us
    pallas_call x1, Pallas kernels: 138 us -> 133 us  [whole_step(): pl.pallas_call(step_kernel, out_shape=(grads, grads, jax.ShapeDtypeStruct...]
where the time goes in v5:
time: 139 us
  Pallas kernels  133 us (96%)
  other arithmetic  4.21 us (3%)
    pallas_call x1, Pallas kernels, whole_step(): pl.pallas_call(step_kernel, out_shape=(grads, grads, jax.ShapeDtypeStruct...  133 us
    convert_element_type x1, other arithmetic, scaled(): return (total.astype(F32) * scale).astype(BF)  4.21 us

profile of v5, /device:TPU:1, one launch (start us, length us, event | category | flops | bytes accessed | tf_op | source)
XLA Modules:
  0.0 138.7 jit_solution(16949149831469942177)
XLA Ops:
  0.6 133.1 %whole_step.1 = (bf16[3,512,512]{2,1,0:T(8,128)(2,1)}, bf16[3,512,512]{2,1,0:T(8,128)(2,1)}, bf16[256,512]{1,0:T(8,128)(2,1)}) custom-call(s32[2,4]{1,0:T(2,128)} %col_in.1, s32[2,256]{1,0:T(2,128)} %bitcast.3, s32[1,256]{1,0:T(1,128)} %cnt_in.1, bf16[2,4,128,128]{3,2,1,0:T(8,128)(2,1)} %val_in.1, bf16[256,512]{1,0:T(8,128)(2,1)} %feat_in.1, ...), custom_call_target="tpu_custom_call" | custom-call | tf_op jit(solution)/shard_map/whole_step/pallas_call | solution.py:469
  133.7 0.0 copy-start
  133.8 4.2 %multiply_convert_fusion = (bf16[3,512,512]{2,1,0:T(8,128)(2,1)}, bf16[3,512,512]{2,1,0:T(8,128)(2,1)}) fusion(bf16[3,512,512]{2,1,0:T(8,128)(2,1)} %get-tuple-element.7, bf16[3,512,512]{2,1,0:T(8,128)(2,1)} %get-tuple-element.6), kind=kLoop, calls=%fused_computation | loop fusion | flops 4718592 | bytes 6291456 | tf_op jit(solution)/shard_map/convert_element_type | solution.py:542
  138.0 0.0 copy-done
  138.0 0.7 copy.12
Async XLA Ops:
  133.7 4.2 %copy-start = (bf16[256,512]{1,0:T(8,128)(2,1)S(1)}, bf16[256,512]{1,0:T(8,128)(2,1)}, u32[]{:S(2)}) copy-start(bf16[256,512]{1,0:T(8,128)(2,1)} %get-tuple-element.16) | copy-start | bytes 786436
